TPU v7x, 256 devices: a whole 4x4x8 slice. The times are simulated.
256 devices in a mesh: graph: 32 (over y, z_lo, core), chan: 8 (over x, z_hi).
Axes of the slice: x: 4, y: 4, z: 8 (z_hi: 2, z_lo: 4; z = z_hi * 4 + z_lo), core: 2. Of those that a mesh axis runs over, the one named last changes fastest.
Arguments:
- embed: bfloat16 [25, 512, 4096], P(None, 'chan', 'graph'), may hold values from -200 to 200
- gain: float32 [5, 512], P(None, 'chan'), may hold values from 0.25 to 1.75
- w_zero: bfloat16 [5, 512, 2560], P(None, 'chan'), may hold values from -0.125 to 0.125
- w_one: bfloat16 [2, 4, 512, 2048], P(None, None, 'chan'), may hold values from -0.125 to 0.125
- w_two: bfloat16 [2, 3, 512, 1536], P(None, None, 'chan'), may hold values from -0.15625 to 0.15625
- rot_table: float32 [19, 25, 256], replicated, may hold values from -1 to 1, as said below
- face_atoms: int32 [1024], P('graph'), may hold values from 0 to 127, as said below
- edge_source: int32 [4096], P('graph'), may hold values from 0 to 159
- edge_target: int32 [4096], P('graph'), may hold values from 0 to 127
- rot_index: int32 [4096], P('graph'), may hold values from 0 to 255
- edge_weight: float32 [4096], P('graph'), may hold values from 0.2 to 1
- cotangent: bfloat16 [25, 512, 4096], P(None, 'chan', 'graph'), may hold values from -1.5 to 1.5
Outputs:
- update: bfloat16 [25, 512, 4096], P(None, 'chan', 'graph')
- grad_embed: bfloat16 [25, 512, 4096], P(None, 'chan', 'graph')
- grad_zero: float32 [5, 512, 2560], P(None, 'chan', 'graph')
- grad_one: float32 [2, 4, 512, 2048], P(None, None, 'chan', 'graph')
- grad_two: float32 [2, 3, 512, 1536], P(None, None, 'chan', 'graph')
Inputs may be any that keep to these rules, and one draw needn't show every extreme that they name: `rot_table`: for every rotation, frame row (m, l) is nonzero only on the 2l + 1 coefficients of degree l, where it is row l + m of an orthogonal (2l + 1)-square matrix shared by the rows of that degree; the degree-0 entry is 1. `face_atoms`: block b holds 32 distinct atom indices counted from the first atom of block b: the first 16 lie at the face toward block b - 1, the last 16 at the face toward block b + 1. `edge_source`: read as in the step that defines src. `edge_target`: counted from the first atom of the edge's block.
All inputs are finite; a program needn't handle non-finite values.
Results may differ from a plain program's by a relative error of at most 0.0062.
Values may be sent and summed in bfloat16 or wider, within the bound.
A program may use at most 128 MiB of HBM per device.

v0:
```python
import jax
import jax.numpy as jnp
from jax import lax
from jax.sharding import Mesh
from jax.sharding import PartitionSpec as P

C = 512
CHAN = ("chan_0", "chan_1")


EPSILON = 1e-06
HIGHEST = lax.Precision.HIGHEST
FRAME = (
    (0, 0),
    (1, 0),
    (2, 0),
    (3, 0),
    (4, 0),
    (1, 1),
    (2, 1),
    (3, 1),
    (4, 1),
    (1, -1),
    (2, -1),
    (3, -1),
    (4, -1),
    (2, 2),
    (3, 2),
    (4, 2),
    (2, -2),
    (3, -2),
    (4, -2),
)


def with_halo(block, sides, width):
    for axis, dim in sides:
        count = lax.axis_size(axis)
        forward = [(i, i + 1) for i in range(count - 1)]
        forward.append((count - 1, 0))
        backward = [(target, source) for source, target in forward]
        low = lax.ppermute(
            lax.slice_in_dim(block, block.shape[dim] - width, None, axis=dim), axis, forward
        )
        high = lax.ppermute(lax.slice_in_dim(block, 0, width, axis=dim), axis, backward)
        block = jnp.concatenate([low, block, high], axis=dim)
    return block


def in_order(parts, dim):
    parts = jnp.moveaxis(parts, 0, dim)
    shape = parts.shape
    return parts.reshape(*shape[:dim], shape[dim] * shape[dim + 1], *shape[dim + 2 :])


def copy_for_each(shard, axis):
    peers = lax.axis_size(axis)
    return lax.all_to_all(
        jnp.broadcast_to(shard[None], (peers, *shard.shape)), axis, 0, 0, tiled=True
    )


def gathered_copies(shard, axis, dim):
    return in_order(copy_for_each(shard, axis), dim)


def cut_along(shard, dim, peers):
    before, after = (shard.shape[:dim], shard.shape[dim + 1 :])
    return jnp.moveaxis(shard.reshape(*before, peers, -1, *after), dim, 0)


def one_scatter(arrays, axis, dims):
    peers = lax.axis_size(axis)
    parts = [cut_along(a, dim, peers) for a, dim in zip(arrays, dims)]
    lines = jnp.concatenate([b.reshape(peers, -1) for b in parts], axis=1)
    extent = max(16, -(-lines.shape[1] // 1024) * 8)
    lines = jnp.pad(lines, ((0, 0), (0, extent * 128 - lines.shape[1]))).reshape(-1, 128)
    ravelled, at, finished = (lax.psum_scatter(lines, axis, tiled=True).reshape(-1), 0, [])
    for b in parts:
        part = b[0]
        finished.append(ravelled[at : at + part.size].reshape(part.shape))
        at += part.size
    return tuple(finished)


def sum_by_axis(shard, axes, dim):
    if not axes:
        return shard
    nearer = lax.psum_scatter(shard, axes[0], scatter_dimension=dim, tiled=True)
    return sum_by_axis(nearer, axes[1:], dim)


def of_everyone(shard, axis):
    everything = copy_for_each(shard, axis)
    return jnp.sum(everything, axis=0)


def gain_rows(gain):
    pieces = [
        jnp.broadcast_to(gain[degree : degree + 1], (2 * degree + 1, gain.shape[1]))
        for degree in range(5)
    ]
    return jnp.concatenate(pieces, axis=0)


def product(left, right):
    return jnp.dot(left, right, preferred_element_type=jnp.float32)


def across(left, right):
    return lax.dot_general(
        left, right, (((0,), (0,)), ((), ())), preferred_element_type=jnp.float32
    )


def outer(left, right):
    return lax.dot_general(
        left, right, (((1,), (1,)), ((), ())), preferred_element_type=jnp.float32
    )


def stack_frame(parts, width, edges):
    row_counts = (5, 4, 4, 3, 3)
    return jnp.concatenate(
        [part.reshape(rows, width, edges) for part, rows in zip(parts, row_counts)], axis=0
    )


def rotate_in(values, rotations):
    rows = []
    for row, pair in enumerate(FRAME):
        first = pair[0] * pair[0]
        total = rotations[row, first][None, :] * values[first].astype(jnp.float32)
        for column in range(first + 1, first + 2 * pair[0] + 1):
            total = total + rotations[row, column][None, :] * values[column].astype(jnp.float32)
        rows.append(total)
    return jnp.stack(rows)


def rotate_out(values, rotations):
    columns = []
    for degree in range(5):
        members = [row for row, pair in enumerate(FRAME) if pair[0] == degree]
        for column in range(degree * degree, (degree + 1) * (degree + 1)):
            total = rotations[members[0], column][None, :] * values[members[0]]
            for row in members[1:]:
                total = total + rotations[row, column][None, :] * values[row]
            columns.append(total)
    return jnp.stack(columns)


def mix_part(w_zero, w_one, w_two, piece):
    count = piece.shape[1]
    edges = piece.shape[2]
    outputs = w_zero.shape[1]

    def columns(weight, blocks):
        shaped = weight.reshape(blocks * outputs, blocks, weight.shape[-1] // blocks)
        return shaped.reshape(blocks * outputs, blocks * count)

    def frame_rows(first, blocks):
        return piece[first : first + blocks].reshape(blocks * count, edges)

    parts = [product(columns(w_zero, 5), frame_rows(0, 5))]
    for weights, first, blocks in ((w_one, 5, 4), (w_two, 13, 3)):
        real_part = columns(weights[0], blocks)
        imag_part = columns(weights[1], blocks)
        plus = frame_rows(first, blocks)
        minus = frame_rows(first + blocks, blocks)
        parts.append(product(real_part, plus) - product(imag_part, minus))
        parts.append(product(real_part, minus) + product(imag_part, plus))
    return tuple(parts)


def mix_backward(w_zero, w_one, w_two, grads, frame):
    outputs = grads.shape[1]
    width = frame.shape[1]
    edges = grads.shape[2]

    def grad_rows(first, blocks):
        return grads[first : first + blocks].reshape(blocks * outputs, edges)

    def frame_rows(first, blocks):
        return frame[first : first + blocks].reshape(blocks * width, edges)

    zero_weight = w_zero.reshape(5 * outputs, 5 * width)
    grad_first = grad_rows(0, 5)
    back = [across(zero_weight, grad_first)]
    weight_zero = outer(grad_first, frame_rows(0, 5)).reshape(5, outputs, 5 * width)
    pairs = []
    for weights, first, blocks in ((w_one, 5, 4), (w_two, 13, 3)):
        real_part = weights[0].reshape(blocks * outputs, blocks * width)
        imag_part = weights[1].reshape(blocks * outputs, blocks * width)
        grad_plus = grad_rows(first, blocks)
        grad_minus = grad_rows(first + blocks, blocks)
        frame_plus = frame_rows(first, blocks)
        frame_minus = frame_rows(first + blocks, blocks)
        back.append(across(real_part, grad_plus) + across(imag_part, grad_minus))
        back.append(across(real_part, grad_minus) - across(imag_part, grad_plus))
        real_grad = outer(grad_plus, frame_plus) + outer(grad_minus, frame_minus)
        imag_grad = outer(grad_minus, frame_plus) - outer(grad_plus, frame_minus)
        pairs.append(
            jnp.stack(
                [
                    real_grad.reshape(blocks, outputs, blocks * width),
                    imag_grad.reshape(blocks, outputs, blocks * width),
                ]
            )
        )
    return (stack_frame(back, width, edges), weight_zero, pairs[0], pairs[1])


def shards(
    embed,
    gain,
    w_zero,
    w_one,
    w_two,
    rot_table,
    face_atoms,
    edge_source,
    edge_target,
    rot_index,
    edge_weight,
    cotangent,
):
    atoms = embed.shape[2]
    local = embed.shape[1]
    halo = face_atoms.shape[0] // 2
    edges = edge_source.shape[0]
    values = embed.astype(jnp.float32)
    gains = gain_rows(gain)
    squares = lax.psum(jnp.sum(values * values, axis=(0, 1)), CHAN)
    inverse = lax.rsqrt(squares / (25 * C) + EPSILON)
    normed = (values * inverse[None, None, :] * gains[:, :, None]).astype(jnp.bfloat16)
    faces = jnp.take(normed, face_atoms, axis=2)
    beside_all = with_halo(faces, (("graph", 2),), halo)
    table = jnp.concatenate([normed, beside_all[:, :, :halo], beside_all[:, :, 3 * halo :]], axis=2)
    rotations = jnp.take(rot_table, rot_index, axis=2)
    own = rotate_in(jnp.take(table, edge_source, axis=2), rotations).astype(jnp.bfloat16)
    piece = gathered_copies(own, CHAN, 1)
    fresh = mix_part(w_zero, w_one, w_two, piece)
    totals = tuple((extra for extra in fresh))
    mixed = stack_frame(totals, local, edges)
    message = rotate_out(mixed * edge_weight[None, None, :], rotations).astype(jnp.bfloat16)
    landing = (edge_target[:, None] == jnp.arange(atoms, dtype=jnp.int32)[None, :]).astype(
        jnp.bfloat16
    )
    update = (
        product(message.reshape(25 * local, edges), landing)
        .reshape(25, local, atoms)
        .astype(jnp.bfloat16)
    )
    arriving = jnp.take(cotangent, edge_target, axis=2)
    grads = (rotate_in(arriving, rotations) * edge_weight[None, None, :]).astype(jnp.bfloat16)
    back, part_zero, part_one, part_two = mix_backward(w_zero, w_one, w_two, grads, piece)
    grad_zero, grad_one, grad_two = one_scatter((part_zero, part_one, part_two), "graph", (2, 3, 3))
    spread = rotate_out(back, rotations)
    leaving = (
        edge_source[:, None] == jnp.arange(atoms + 2 * halo, dtype=jnp.int32)[None, :]
    ).astype(jnp.float32)
    collected = jnp.dot(
        spread.reshape(25 * C, edges),
        leaving,
        precision=HIGHEST,
        preferred_element_type=jnp.float32,
    ).reshape(25, C, atoms + 2 * halo)
    mine = sum_by_axis(collected, CHAN, 1)
    returned = with_halo(mine[:, :, atoms:], (("graph", 2),), halo)
    incoming = jnp.concatenate([returned[:, :, :halo], returned[:, :, 3 * halo :]], axis=2)
    owners = (face_atoms[:, None] == jnp.arange(atoms, dtype=jnp.int32)[None, :]).astype(
        jnp.float32
    )
    settled = jnp.dot(
        incoming.reshape(25 * local, 2 * halo),
        owners,
        precision=HIGHEST,
        preferred_element_type=jnp.float32,
    )
    grad_normed = mine[:, :, :atoms] + settled.reshape(25, local, atoms)
    tally = of_everyone(jnp.sum(values * gains[:, :, None] * grad_normed, axis=(0, 1)), CHAN)
    grad_embed = (
        inverse[None, None, :] * gains[:, :, None] * grad_normed
        - values * (inverse**3 * tally / (25 * C))[None, None, :]
    ).astype(jnp.bfloat16)
    return (update, grad_embed, grad_zero, grad_one, grad_two)


def solution(mesh):
    torus = Mesh(mesh.devices.reshape(mesh.shape["graph"], 4, 2), ("graph", "chan_0", "chan_1"))
    return jax.shard_map(
        shards,
        mesh=torus,
        in_specs=(
            P(None, CHAN, "graph"),
            P(None, CHAN),
            P(None, CHAN, None),
            P(None, None, CHAN, None),
            P(None, None, CHAN, None),
            P(),
            P("graph"),
            P("graph"),
            P("graph"),
            P("graph"),
            P("graph"),
            P(None, CHAN, "graph"),
        ),
        out_specs=(
            P(None, CHAN, "graph"),
            P(None, CHAN, "graph"),
            P(None, CHAN, "graph"),
            P(None, None, CHAN, "graph"),
            P(None, None, CHAN, "graph"),
        ),
        check_vma=False,
    )
```

profile of v0, /device:TPU:1, one launch (start us, length us, event | category | flops | bytes accessed | tf_op | source)
XLA Modules:
  0.0 882.6 jit_solution(17725810651768906155)
XLA Ops:
  10.0 3.1 copy.110
  13.1 2.5 gather_fusion
  16.9 10.3 %slice_reduce_fusion.98 = (f32[128]{0:T(128)S(1)}, f32[128]{0:T(128)S(1)}, f32[128]{0:T(128)S(1)}, f32[128]{0:T(128)S(1)}, f32[128]{0:T(128)S(1)}, /*index=5*/f3...) fusion(f32[19,25,128]{1,0,2:T(8,128)S(1)} %select_bitcast_fusion), kind=kLoop, calls=%fused_computation.248 | loop fusion | bytes 19456 | tf_op jit(solution)/shard_map/slice | solution.py:133
  27.3 10.4 %slice_reduce_fusion.81 = (f32[128]{0:T(128)}, f32[128]{0:T(128)S(1)}, f32[128]{0:T(128)S(1)}, f32[128]{0:T(128)}, f32[128]{0:T(128)}, /*index=5*/f32[128]{0:T(1...) fusion(f32[19,25,128]{1,0,2:T(8,128)S(1)} %select_bitcast_fusion), kind=kLoop, calls=%fused_computation.231 | loop fusion | bytes 19456 | tf_op jit(solution)/shard_map/slice | solution.py:133
  37.7 10.0 %slice_reduce_fusion.57 = (f32[128]{0:T(128)}, f32[128]{0:T(128)}, f32[128]{0:T(128)}, f32[128]{0:T(128)}, f32[128]{0:T(128)}, /*index=5*/f32[128]{0:T(128)}, f3...) fusion(f32[19,25,128]{1,0,2:T(8,128)S(1)} %select_bitcast_fusion), kind=kLoop, calls=%fused_computation.207 | loop fusion | bytes 19456 | tf_op jit(solution)/shard_map/slice | solution.py:133
  47.8 10.4 %slice_reduce_fusion.41 = (f32[128]{0:T(128)}, f32[128]{0:T(128)}, f32[128]{0:T(128)}, f32[128]{0:T(128)}, f32[128]{0:T(128)S(1)}, /*index=5*/f32[128]{0:T(128)S...) fusion(f32[19,25,128]{1,0,2:T(8,128)S(1)} %select_bitcast_fusion), kind=kLoop, calls=%fused_computation.191 | loop fusion | bytes 19456 | tf_op jit(solution)/shard_map/slice | solution.py:133
  58.2 10.8 %slice_reduce_fusion.20 = (f32[128]{0:T(128)}, f32[128]{0:T(128)}, f32[128]{0:T(128)S(1)}, f32[128]{0:T(128)S(1)}, f32[128]{0:T(128)S(1)}, /*index=5*/f32[128]{0...) fusion(f32[19,25,128]{1,0,2:T(8,128)S(1)} %select_bitcast_fusion), kind=kLoop, calls=%fused_computation.170 | loop fusion | bytes 19456 | tf_op jit(solution)/shard_map/slice | solution.py:133
  69.0 10.3 %slice_reduce_fusion.8 = (f32[128]{0:T(128)}, f32[128]{0:T(128)}, f32[128]{0:T(128)}, f32[128]{0:T(128)}, f32[128]{0:T(128)}, /*index=5*/f32[128]{0:T(128)}, f32...) fusion(f32[19,25,128]{1,0,2:T(8,128)S(1)} %select_bitcast_fusion), kind=kLoop, calls=%fused_computation.158 | loop fusion | bytes 19456 | tf_op jit(solution)/shard_map/slice | solution.py:133
  79.2 1.6 copy.118
  80.9 1.7 gather_fusion.3
  82.5 2.1 copy.119
  120.4 6.2 fusion.19
  126.7 85.3 %reduce-scatter.5.cloned.1.call-done = f32[25,128,160]{1,2,0:T(8,128)} async-done(((f32[25,512,160]{1,2,0:T(8,128)}), f32[25,128,160]{1,2,0:T(8,128)}) %reduce-scatter.5.cloned.1.call-update) | async-done | bytes 2048016 | tf_op jit(solution)/shard_map/reduce_scatter | solution.py:89
  211.9 4.9 copy.130
  216.9 5.0 reshape.2590
  223.6 62.1 %reduce-scatter.7.cloned.1.call-done = f32[64,4000]{1,0:T(8,128)} async-done(((f32[128,4000]{1,0:T(8,128)}), f32[64,4000]{1,0:T(8,128)}) %reduce-scatter.7.cloned.1.call-update) | async-done | bytes 1024016
  285.7 3.2 reshape.2591
  288.9 3.3 fusion.244
  292.3 2.3 copy.135
  295.7 2.3 copy.134
  299.6 1.3 slice.941
  301.9 3.5 fusion.10
  306.0 4.0 all-to-all-start.1
  311.2 27.8 %psum.7 = f32[128]{0:T(128)S(1)} all-reduce(f32[128]{0:T(128)S(1)} %get-tuple-element.155), channel_id=1, replica_groups=mesh['graph'=32,'chan_0'=4,'chan_1'=2] {'chan_0','chan_1'}, use_global_device_ids=true, to_apply=%region_1.0 | all-reduce | flops 128 | bytes 1024 | tf_op jit(solution)/shard_map/psum | solution.py:233
  339.0 2.5 fusion.12
  341.6 3.3 copy.111
  344.9 1.9 gather_fusion.1
  349.4 10.1 %collective-permute-start.1 = (bf16[25,64,16]{2,1,0:T(8,128)(2,1)S(1)}, bf16[25,64,16]{2,1,0:T(8,128)(2,1)S(1)}, u32[]{:S(2)}, u32[]{:S(2)}) collective-permute-start(bf16[25,64,16]{2,1,0:T(8,128)(2,1)S(1)} %get-tuple-element.169), channel_id=1, source_target_pairs={{8,0},{16,8},{24,16},{32,24},{40,32},{48,40},{56,48},{64,56},{72,6... | collective-permute-start | bytes 153608 | tf_op jit(solution)/shard_map/ppermute | solution.py:45
  360.2 1.9 collective-permute-done.1
  362.1 6.5 collective-permute-done
  368.6 2.2 pad_maximum_fusion.1
  370.8 3.0 copy.113
  373.7 3.0 gather_fusion.2
  376.7 2.8 copy.114
  393.0 58.8 %all_to_all.11 = bf16[8,19,64,128]{3,2,1,0:T(8,128)(2,1)S(1)} all-to-all(bf16[8,19,64,128]{3,2,1,0:T(8,128)(2,1)S(1)} %broadcast_in_dim.117), channel_id=1, replica_groups=mesh['graph'=32,'chan_0'=4,'chan_1'=2] {'chan_0','chan_1'}, dimensions={0} | all-to-all | bytes 4980736 | tf_op jit(solution)/shard_map/all_to_all | solution.py:58
  454.9 1.3 fusion.258
  456.2 1.8 fusion.257
  458.0 1.8 fusion.256
  459.8 1.4 convolution_subtract_fusion.1
  461.2 3.6 stack.195
  464.7 2.7 convolution_add_fusion.1
  467.5 3.6 stack.194
  471.1 3.6 maximum_bitcast_fusion.1
  474.7 6.3 copy.126
  481.0 7.4 reshape.2543
  488.4 3.6 convolution_subtract_fusion
  491.9 5.0 stack.192
  497.0 6.8 copy.125
  503.8 1.8 convolution_add_fusion
  505.6 4.8 stack.191
  510.4 4.8 copy.124
  515.2 4.2 maximum_bitcast_fusion
  519.4 6.9 reshape.2542
  526.4 2.0 convolution_bitcast_fusion.1
  528.4 3.1 copy.123
  531.5 6.4 reshape.2541
  537.8 8.1 pad_maximum_fusion
  546.0 8.5 reshape.2544
  556.4 1.9 fusion.250
  558.3 1.5 fusion.5
  559.9 1.9 fusion.251
  561.8 1.5 fusion.4
  564.1 1.7 fusion.260
  585.5 285.1 %all-reduce.3.cloned.1.call-done = f32[19200,128]{1,0:T(8,128)} async-done(((f32[19200,128]{1,0:T(8,128)}), f32[19200,128]{1,0:T(8,128)}) %all-reduce.3.cloned.1.call-update) | async-done | bytes 9830416
  (438 shorter events, 92.1 us)
Async XLA Ops:
  7.2 89.3 %copy-start = (bf16[5,64,2560]{2,1,0:T(8,128)(2,1)S(1)}, bf16[5,64,2560]{2,1,0:T(8,128)(2,1)}, u32[]{:S(2)}) copy-start(bf16[5,64,2560]{2,1,0:T(8,128)(2,1)} %param.14) | copy-start | bytes 4915204
  7.2 204.8 %reduce-scatter.5.cloned.1.call-start = ((), (), s32[]{:S(2)}) async-start(), calls=%async_computation.4 | async-start | bytes 10240000 | tf_op jit(solution)/shard_map/reduce_scatter | solution.py:89
  15.9 63.4 %copy-start.24 = (bf16[25,64,128]{2,1,0:T(8,128)(2,1)S(1)}, bf16[25,64,128]{2,1,0:T(8,128)(2,1)}, u32[]{:S(2)}) copy-start(bf16[25,64,128]{2,1,0:T(8,128)(2,1)} %param.23) | copy-start | bytes 1228804
  16.9 80.1 %copy-start.124 = (f32[128]{0:T(128)}, f32[128]{0:T(128)S(1)}, u32[]{:S(2)}) copy-start(f32[128]{0:T(128)S(1)} %slice_reduce_fusion.114) | copy-start | bytes 1540
  27.2 73.2 %copy-start.121 = (f32[128]{0:T(128)}, f32[128]{0:T(128)S(1)}, u32[]{:S(2)}) copy-start(f32[128]{0:T(128)S(1)} %get-tuple-element.151) | copy-start | bytes 1540
  27.2 80.5 %copy-start.109 = (f32[128]{0:T(128)}, f32[128]{0:T(128)S(1)}, u32[]{:S(2)}) copy-start(f32[128]{0:T(128)S(1)} %get-tuple-element.144) | copy-start | bytes 1540
  27.2 81.4 %copy-start.94 = (f32[128]{0:T(128)}, f32[128]{0:T(128)S(1)}, u32[]{:S(2)}) copy-start(f32[128]{0:T(128)S(1)} %get-tuple-element.143) | copy-start | bytes 1540
  27.2 82.2 %copy-start.82 = (f32[128]{0:T(128)}, f32[128]{0:T(128)S(1)}, u32[]{:S(2)}) copy-start(f32[128]{0:T(128)S(1)} %get-tuple-element.142) | copy-start | bytes 1540
  27.2 83.1 %copy-start.73 = (f32[128]{0:T(128)}, f32[128]{0:T(128)S(1)}, u32[]{:S(2)}) copy-start(f32[128]{0:T(128)S(1)} %get-tuple-element.141) | copy-start | bytes 1540
  27.2 83.9 %copy-start.64 = (f32[128]{0:T(128)}, f32[128]{0:T(128)S(1)}, u32[]{:S(2)}) copy-start(f32[128]{0:T(128)S(1)} %get-tuple-element.140) | copy-start | bytes 1540
  27.2 84.8 %copy-start.55 = (f32[128]{0:T(128)}, f32[128]{0:T(128)S(1)}, u32[]{:S(2)}) copy-start(f32[128]{0:T(128)S(1)} %get-tuple-element.139) | copy-start | bytes 1540
  27.2 85.6 %copy-start.46 = (f32[128]{0:T(128)}, f32[128]{0:T(128)S(1)}, u32[]{:S(2)}) copy-start(f32[128]{0:T(128)S(1)} %get-tuple-element.135) | copy-start | bytes 1540
  27.2 86.4 %copy-start.40 = (f32[128]{0:T(128)}, f32[128]{0:T(128)S(1)}, u32[]{:S(2)}) copy-start(f32[128]{0:T(128)S(1)} %get-tuple-element.138) | copy-start | bytes 1540
  27.2 87.3 %copy-start.31 = (f32[128]{0:T(128)}, f32[128]{0:T(128)S(1)}, u32[]{:S(2)}) copy-start(f32[128]{0:T(128)S(1)} %get-tuple-element.137) | copy-start | bytes 1540
  37.7 72.6 %copy-start.115 = (f32[128]{0:T(128)}, f32[128]{0:T(128)S(1)}, u32[]{:S(2)}) copy-start(f32[128]{0:T(128)S(1)} %get-tuple-element.118) | copy-start | bytes 1540
  37.7 73.4 %copy-start.100 = (f32[128]{0:T(128)}, f32[128]{0:T(128)S(1)}, u32[]{:S(2)}) copy-start(f32[128]{0:T(128)S(1)} %get-tuple-element.117) | copy-start | bytes 1540
  37.7 78.5 %copy-start.34 = (f32[128]{0:T(128)}, f32[128]{0:T(128)S(1)}, u32[]{:S(2)}) copy-start(f32[128]{0:T(128)S(1)} %get-tuple-element.134) | copy-start | bytes 1540
  37.7 79.4 %copy-start.25 = (f32[128]{0:T(128)}, f32[128]{0:T(128)S(1)}, u32[]{:S(2)}) copy-start(f32[128]{0:T(128)S(1)} %get-tuple-element.133) | copy-start | bytes 1540
  47.7 64.3 %copy-start.118 = (f32[128]{0:T(128)}, f32[128]{0:T(128)S(1)}, u32[]{:S(2)}) copy-start(f32[128]{0:T(128)S(1)} %get-tuple-element.115) | copy-start | bytes 1540
  47.7 65.2 %copy-start.103 = (f32[128]{0:T(128)}, f32[128]{0:T(128)S(1)}, u32[]{:S(2)}) copy-start(f32[128]{0:T(128)S(1)} %get-tuple-element.114) | copy-start | bytes 1540
  47.7 66.0 %copy-start.88 = (f32[128]{0:T(128)}, f32[128]{0:T(128)S(1)}, u32[]{:S(2)}) copy-start(f32[128]{0:T(128)S(1)} %get-tuple-element.113) | copy-start | bytes 1540
  47.7 66.8 %copy-start.76 = (f32[128]{0:T(128)}, f32[128]{0:T(128)S(1)}, u32[]{:S(2)}) copy-start(f32[128]{0:T(128)S(1)} %get-tuple-element.112) | copy-start | bytes 1540
  47.7 67.6 %copy-start.67 = (f32[128]{0:T(128)}, f32[128]{0:T(128)S(1)}, u32[]{:S(2)}) copy-start(f32[128]{0:T(128)S(1)} %get-tuple-element.111) | copy-start | bytes 1540
  47.7 68.5 %copy-start.58 = (f32[128]{0:T(128)}, f32[128]{0:T(128)S(1)}, u32[]{:S(2)}) copy-start(f32[128]{0:T(128)S(1)} %get-tuple-element.110) | copy-start | bytes 1540
  47.7 69.4 %copy-start.49 = (f32[128]{0:T(128)}, f32[128]{0:T(128)S(1)}, u32[]{:S(2)}) copy-start(f32[128]{0:T(128)S(1)} %get-tuple-element.109) | copy-start | bytes 1540
  47.7 70.2 %copy-start.43 = (f32[128]{0:T(128)}, f32[128]{0:T(128)S(1)}, u32[]{:S(2)}) copy-start(f32[128]{0:T(128)S(1)} %get-tuple-element.108) | copy-start | bytes 1540
  47.7 71.0 %copy-start.37 = (f32[128]{0:T(128)}, f32[128]{0:T(128)S(1)}, u32[]{:S(2)}) copy-start(f32[128]{0:T(128)S(1)} %get-tuple-element.107) | copy-start | bytes 1540
  47.7 71.9 %copy-start.28 = (f32[128]{0:T(128)}, f32[128]{0:T(128)S(1)}, u32[]{:S(2)}) copy-start(f32[128]{0:T(128)S(1)} %get-tuple-element.106) | copy-start | bytes 1540
  58.2 57.1 %copy-start.106 = (f32[128]{0:T(128)}, f32[128]{0:T(128)S(1)}, u32[]{:S(2)}) copy-start(f32[128]{0:T(128)S(1)} %get-tuple-element.87) | copy-start | bytes 1540
  58.2 58.0 %copy-start.91 = (f32[128]{0:T(128)}, f32[128]{0:T(128)S(1)}, u32[]{:S(2)}) copy-start(f32[128]{0:T(128)S(1)} %get-tuple-element.86) | copy-start | bytes 1540
  58.2 58.9 %copy-start.79 = (f32[128]{0:T(128)}, f32[128]{0:T(128)S(1)}, u32[]{:S(2)}) copy-start(f32[128]{0:T(128)S(1)} %get-tuple-element.85) | copy-start | bytes 1540
  58.2 59.7 %copy-start.70 = (f32[128]{0:T(128)}, f32[128]{0:T(128)S(1)}, u32[]{:S(2)}) copy-start(f32[128]{0:T(128)S(1)} %get-tuple-element.84) | copy-start | bytes 1540
  58.2 60.6 %copy-start.61 = (f32[128]{0:T(128)}, f32[128]{0:T(128)S(1)}, u32[]{:S(2)}) copy-start(f32[128]{0:T(128)S(1)} %get-tuple-element.83) | copy-start | bytes 1540
  58.2 61.4 %copy-start.52 = (f32[128]{0:T(128)}, f32[128]{0:T(128)S(1)}, u32[]{:S(2)}) copy-start(f32[128]{0:T(128)S(1)} %get-tuple-element.82) | copy-start | bytes 1540
  69.0 48.9 %copy-start.112 = (f32[128]{0:T(128)}, f32[128]{0:T(128)S(1)}, u32[]{:S(2)}) copy-start(f32[128]{0:T(128)S(1)} %get-tuple-element.63) | copy-start | bytes 1540
  69.0 49.8 %copy-start.97 = (f32[128]{0:T(128)}, f32[128]{0:T(128)S(1)}, u32[]{:S(2)}) copy-start(f32[128]{0:T(128)S(1)} %get-tuple-element.62) | copy-start | bytes 1540
  69.0 50.7 %copy-start.85 = (f32[128]{0:T(128)}, f32[128]{0:T(128)S(1)}, u32[]{:S(2)}) copy-start(f32[128]{0:T(128)S(1)} %get-tuple-element.61) | copy-start | bytes 1540
  126.6 159.1 %reduce-scatter.7.cloned.1.call-start = ((), (), s32[]{:S(2)}) async-start(), calls=%async_computation.5 | async-start | bytes 3145728
  294.6 6.3 collective-permute-start.3
  298.0 3.9 collective-permute-start.2
  306.0 33.0 %all-to-all-start.1 = ((f32[8,1,128]{2,1,0:T(1,128)}), f32[8,1,128]{2,1,0:T(1,128)S(1)}, u32[]{:S(2)}, u32[]{:S(2)}) async-start(f32[8,1,128]{2,1,0:T(1,128)} %broadcast_in_dim.120), calls=%async_computation.2 | async-start | bytes 8192 | tf_op jit(solution)/shard_map/all_to_all | solution.py:58
  309.9 560.7 %all-reduce.3.cloned.1.call-start = ((), (), s32[]{:S(2)}) async-start(), calls=%async_computation.6 | async-start | bytes 19660800
  349.0 32.9 %copy-start.56 = (f32[128]{0:T(128)S(1)}, f32[128]{0:T(128)}, u32[]{:S(2)}) copy-start(f32[128]{0:T(128)} %copy-done.55) | copy-start | bytes 1540
  349.0 32.9 %copy-start.65 = (f32[128]{0:T(128)S(1)}, f32[128]{0:T(128)}, u32[]{:S(2)}) copy-start(f32[128]{0:T(128)} %copy-done.64) | copy-start | bytes 1540
  349.0 32.9 %copy-start.74 = (f32[128]{0:T(128)S(1)}, f32[128]{0:T(128)}, u32[]{:S(2)}) copy-start(f32[128]{0:T(128)} %copy-done.73) | copy-start | bytes 1540
  349.3 33.4 %copy-start.26 = (f32[128]{0:T(128)S(1)}, f32[128]{0:T(128)}, u32[]{:S(2)}) copy-start(f32[128]{0:T(128)} %copy-done.25) | copy-start | bytes 1540
  349.3 33.4 %copy-start.32 = (f32[128]{0:T(128)S(1)}, f32[128]{0:T(128)}, u32[]{:S(2)}) copy-start(f32[128]{0:T(128)} %copy-done.31) | copy-start | bytes 1540
  349.3 33.4 %copy-start.35 = (f32[128]{0:T(128)S(1)}, f32[128]{0:T(128)}, u32[]{:S(2)}) copy-start(f32[128]{0:T(128)} %copy-done.34) | copy-start | bytes 1540
  349.3 33.4 %copy-start.41 = (f32[128]{0:T(128)S(1)}, f32[128]{0:T(128)}, u32[]{:S(2)}) copy-start(f32[128]{0:T(128)} %copy-done.40) | copy-start | bytes 1540
  349.3 33.4 %copy-start.47 = (f32[128]{0:T(128)S(1)}, f32[128]{0:T(128)}, u32[]{:S(2)}) copy-start(f32[128]{0:T(128)} %copy-done.46) | copy-start | bytes 1540
  349.3 34.9 %copy-start.101 = (f32[128]{0:T(128)S(1)}, f32[128]{0:T(128)}, u32[]{:S(2)}) copy-start(f32[128]{0:T(128)} %copy-done.100) | copy-start | bytes 1540
  349.3 34.9 %copy-start.116 = (f32[128]{0:T(128)S(1)}, f32[128]{0:T(128)}, u32[]{:S(2)}) copy-start(f32[128]{0:T(128)} %copy-done.115) | copy-start | bytes 1540
  349.3 34.9 %copy-start.119 = (f32[128]{0:T(128)S(1)}, f32[128]{0:T(128)}, u32[]{:S(2)}) copy-start(f32[128]{0:T(128)} %copy-done.118) | copy-start | bytes 1540
  349.3 35.6 %copy-start.29 = (f32[128]{0:T(128)S(1)}, f32[128]{0:T(128)}, u32[]{:S(2)}) copy-start(f32[128]{0:T(128)} %copy-done.28) | copy-start | bytes 1540
  349.4 35.6 %copy-start.38 = (f32[128]{0:T(128)S(1)}, f32[128]{0:T(128)}, u32[]{:S(2)}) copy-start(f32[128]{0:T(128)} %copy-done.37) | copy-start | bytes 1540
  349.4 35.6 %copy-start.44 = (f32[128]{0:T(128)S(1)}, f32[128]{0:T(128)}, u32[]{:S(2)}) copy-start(f32[128]{0:T(128)} %copy-done.43) | copy-start | bytes 1540
  349.4 35.6 %copy-start.50 = (f32[128]{0:T(128)S(1)}, f32[128]{0:T(128)}, u32[]{:S(2)}) copy-start(f32[128]{0:T(128)} %copy-done.49) | copy-start | bytes 1540
  349.4 35.6 %copy-start.59 = (f32[128]{0:T(128)S(1)}, f32[128]{0:T(128)}, u32[]{:S(2)}) copy-start(f32[128]{0:T(128)} %copy-done.58) | copy-start | bytes 1540
  349.4 35.6 %copy-start.68 = (f32[128]{0:T(128)S(1)}, f32[128]{0:T(128)}, u32[]{:S(2)}) copy-start(f32[128]{0:T(128)} %copy-done.67) | copy-start | bytes 1540
  349.4 35.6 %copy-start.77 = (f32[128]{0:T(128)S(1)}, f32[128]{0:T(128)}, u32[]{:S(2)}) copy-start(f32[128]{0:T(128)} %copy-done.76) | copy-start | bytes 1540
  349.4 35.6 %copy-start.89 = (f32[128]{0:T(128)S(1)}, f32[128]{0:T(128)}, u32[]{:S(2)}) copy-start(f32[128]{0:T(128)} %copy-done.88) | copy-start | bytes 1540
  349.4 35.6 %copy-start.104 = (f32[128]{0:T(128)S(1)}, f32[128]{0:T(128)}, u32[]{:S(2)}) copy-start(f32[128]{0:T(128)} %copy-done.103) | copy-start | bytes 1540
  349.4 12.7 %collective-permute-start.1 = (bf16[25,64,16]{2,1,0:T(8,128)(2,1)S(1)}, bf16[25,64,16]{2,1,0:T(8,128)(2,1)S(1)}, u32[]{:S(2)}, u32[]{:S(2)}) collective-permute-start(bf16[25,64,16]{2,1,0:T(8,128)(2,1)S(1)} %get-tuple-element.169), channel_id=1, source_target_pairs={{8,0},{16,8},{24,16},{32,24},{40,32},{48,40},{56,48},{64,56},{72,6... | collective-permute-start | bytes 153608 | tf_op jit(solution)/shard_map/ppermute | solution.py:45
  359.5 9.1 %collective-permute-start = (bf16[25,64,16]{2,1,0:T(8,128)(2,1)S(1)}, bf16[25,64,16]{2,1,0:T(8,128)(2,1)S(1)}, u32[]{:S(2)}, u32[]{:S(2)}) collective-permute-start(bf16[25,64,16]{2,1,0:T(8,128)(2,1)S(1)} %get-tuple-element.168), channel_id=1, source_target_pairs={{0,8},{8,16},{16,24},{24,32},{32,40},{40,48},{48,56},{56,64},{64,7... | collective-permute-start | bytes 153608 | tf_op jit(solution)/shard_map/ppermute | solution.py:42
  (79 other events, 1036.2 us)
Sparse Core Ops, SparseCore 0:
  126.7 85.1 reduce-scatter.4
  222.0 63.6 reduce-scatter.6
  554.6 315.9 all-reduce.2
where the time goes:
time: 896 us; the launch traced here: 883 us
  waiting for transfers between devices  442 us (49%)
  local copies, waits for them, and re-layouts  191 us (21%)
  other arithmetic  89.5 us (10%)
  blocking collectives  86.6 us (10%)
  matrix products  40.1 us (4%)
  between operations  17 us (2%)
  starting transfers between devices  16.1 us (2%)
    unnamed x5, waiting for transfers between devices  347 us
    reduce_scatter x1, waiting for transfers between devices, sum_by_axis(): nearer = lax.psum_scatter(shard, axes[0], scatter_dimension=dim, tiled=True)  85.3 us
    slice x6, local copies, waits for them, and re-layouts, rotate_in(): total = rotations[row, first][None, :] * values[first].astype(jnp.float32)  62.1 us
    all_to_all x1, blocking collectives, copy_for_each(): lax.all_to_all(jnp.broadcast_to(shard[None], (peers, *shard.shape)), axis...  58.8 us
    unnamed x84, other arithmetic  56.6 us
    another operation x6, local copies, waits for them, and re-layouts, mix_backward(): jnp.stack([real_grad.reshape(blocks, outputs, blocks * width), imag_grad....  28.6 us
    psum x1, blocking collectives, shards(): squares = lax.psum(jnp.sum(values * values, axis=(0, 1)), CHAN)  27.8 us
    unnamed x283, local copies, waits for them, and re-layouts  25.3 us
  transfers between devices with their start and end apart: 8, of which 6 were waited for; matrix products, arithmetic and copies ran while one was open for 4% of the time, Pallas kernels for 0%

commit v1 on v0

v1 whole, which is shorter than its diff:
```python
import jax
import jax.numpy as jnp
from jax import lax
from jax.experimental import pallas as pl
from jax.experimental.pallas import tpu as pltpu
from jax.sharding import Mesh
from jax.sharding import PartitionSpec as P

C = 512
EPSILON = 1e-06
CHAN = ("x", "zh")
GRAPH = ("y", "z", "core")
DEGREE = (0, 1, 2, 3, 4, 1, 2, 3, 4, 1, 2, 3, 4, 2, 3, 4, 2, 3, 4)
ROWS = tuple(tuple(j for j in range(19) if DEGREE[j] == l) for l in range(5))
F32 = jnp.float32
BF16 = jnp.bfloat16
VMEM_LIMIT = 60 * 1024 * 1024
MESH = pl.DeviceIdType.MESH
PIECES = (slice(0, 10), slice(10, 19))
HALVES = (slice(0, 320), slice(320, 640))


def nt(left, right):
    return lax.dot_general(left, right, (((1,), (1,)), ((), ())), preferred_element_type=F32)


def tn(left, right):
    return lax.dot_general(left, right, (((0,), (0,)), ((), ())), preferred_element_type=F32)


def nn(left, right):
    return jnp.dot(left, right, preferred_element_type=F32)


def hot(index_row, rows, first=0):
    edges = index_row.shape[1]
    row = lax.broadcasted_iota(jnp.int32, (rows, edges), 0) + first
    return jnp.where(row == index_row, 1.0, 0.0).astype(BF16)


def rotate_in(rot, values, j):
    l = DEGREE[j]
    total = None
    for k in range(l * l, (l + 1) * (l + 1)):
        term = rot[j, k : k + 1, :] * values[k]
        total = term if total is None else total + term
    return total


def rotate_out(rot, values, k, l):
    total = None
    for j in ROWS[l]:
        term = rot[j, k : k + 1, :] * values[j]
        total = term if total is None else total + term
    return total


class Net:
    def __init__(self, send, recv):
        self.send, self.recv, self.started = send, recv, []

    def copy(self, source, landing, device):
        at = len(self.started)
        assert at < COPIES
        one = pltpu.make_async_remote_copy(
            src_ref=source,
            dst_ref=landing,
            send_sem=self.send.at[at],
            recv_sem=self.recv.at[at],
            device_id=device,
            device_id_type=MESH,
        )
        one.start()
        self.started.append(one)
        return one

    def finish(self):
        for one in self.started:
            one.wait_send()


COPIES = 83


def layer_kernel(
    embed, cotangent, gain_t, rot_table, face, face_left, face_right,
    source, target, spin, weight, w_zero_hbm, w_one_hbm, w_two_hbm,
    update, grad_embed, sums,
    w_zero, w_one, w_two, faces, halo_t, rot, values, grads, mine, square, squares, every, twin,
    back, relay_left, relay_right, from_left, from_right, to_far, far,
    scaled, scaled_twin, flat_zero, flat_one, flat_two, sel_zero, sel_one, sel_two,
    right_zero, right_one, right_two, part, pass_left, pass_right, up_left, up_right,
    to_line, line, kept, mixed, message, tally, tallies, own, leaving, returned,
    tally_out, tally_in, settled, send, recv, load,
):
    x, h = lax.axis_index("x"), lax.axis_index("zh")
    y, z, core = lax.axis_index("y"), lax.axis_index("z"), lax.axis_index("core")
    xr, xl, xo = lax.rem(x + 1, 4), lax.rem(x + 3, 4), lax.rem(x + 2, 4)
    yr, yl, yo = lax.rem(y + 1, 4), lax.rem(y + 3, 4), lax.rem(y + 2, 4)
    me = y * 8 + z * 2 + core
    ahead, behind = lax.rem(me + 1, 32), lax.rem(me + 31, 32)

    def graph_at(g):
        return {"y": g // 8, "z": lax.rem(g // 2, 4), "core": lax.rem(g, 2)}

    to_xr, to_xl = {"x": xr}, {"x": xl}
    to_yr, to_yl = {"y": yr}, {"y": yl}
    to_far_half = {"zh": 1 - h}
    to_twin = {"core": 1 - core}
    to_ahead, to_behind = graph_at(ahead), graph_at(behind)
    chan_peers = [
        {"x": lax.rem(x + dx, 4), "zh": lax.rem(h + dh, 2)}
        for dx in range(4)
        for dh in range(2)
        if dx or dh
    ]
    line_peers = [None] + [{"z": lax.rem(z + o, 4)} for o in (1, 2, 3)]
    chan = x * 2 + h

    local = embed.shape[1]
    atoms = embed.shape[2]
    edges = source.shape[1]
    count = 25 * local
    net = Net(send, recv)

    loads = [
        pltpu.make_async_copy(a, b, load.at[i])
        for i, (a, b) in enumerate(
            ((w_zero_hbm, w_zero), (w_one_hbm, w_one), (w_two_hbm, w_two))
        )
    ]
    for one in loads:
        one.start()

    barrier = pltpu.get_barrier_semaphore()
    partners = chan_peers + line_peers[1:] + [to_yr, to_yl, to_ahead, to_behind]
    for device in partners:
        pl.semaphore_signal(barrier, inc=1, device_id=device, device_id_type=MESH)

    face_col = lax.broadcasted_iota(jnp.int32, (face.shape[0], atoms), 1)
    face_hot = jnp.where(face_col == face[...], 1.0, 0.0).astype(BF16)
    flat_embed = embed[...].reshape(count, atoms)
    faces[...] = nt(face_hot, flat_embed).astype(BF16)
    pl.semaphore_wait(barrier, len(partners))
    halo = [
        net.copy(faces.at[16:32], halo_t.at[0:16], to_ahead),
        net.copy(faces.at[0:16], halo_t.at[16:32], to_behind),
    ]

    turn = hot(spin[...], rot_table.shape[2])
    for j in range(19):
        line_j = rot_table[j]
        high = line_j.astype(BF16)
        low = (line_j - high.astype(F32)).astype(BF16)
        rot[j] = nn(high, turn) + nn(low, turn)
    total_a = jnp.zeros((1, atoms), F32)
    for k in range(25):
        one = embed[k].astype(F32)
        total_a = total_a + jnp.sum(one * one, axis=0, keepdims=True)
    here = hot(source[...], atoms)
    near = hot(source[...], 32, atoms)

    for one in halo:
        one.wait_recv()
    values[...] = (nn(flat_embed, here) + tn(halo_t[...], near)).reshape(25, local, edges)
    for j in range(19):
        l = DEGREE[j]
        mine[j] = (rotate_in(rot, values, j) * gain_t[:, l : l + 1]).astype(BF16)
    first, second = (
        [mine.at[p] for p in PIECES],
        [every.at[p, chan] for p in PIECES],
    )
    cross = [net.copy(first[p], second[p], to_far_half) for p in (0, 1)]
    near_r = [net.copy(first[p], second[p], to_xr) for p in (0, 1)]
    near_l = [net.copy(first[p], second[p], to_xl) for p in (1, 0)][::-1]
    twins = [net.copy(mine, twin.at[:, chan], to_twin)]
    total_e = jnp.zeros((1, edges), F32)
    for k in range(25):
        one = values[k]
        total_e = total_e + jnp.sum(one * one, axis=0, keepdims=True)
    square[...] = jnp.concatenate([total_e, total_a, jnp.zeros((6, edges), F32)], axis=0)
    asked = [net.copy(square, squares.at[i], d) for i, d in enumerate(chan_peers)]
    for j in range(19):
        every[j, chan] = mine[j]

    arrive = hot(target[...], atoms)
    values[...] = nn(cotangent[...].reshape(count, atoms), arrive).reshape(25, local, edges)
    for j in range(19):
        grads[j] = (rotate_in(rot, values, j) * weight[...]).astype(BF16)

    def forward(p, x_from, h_from, device):
        block = every.at[PIECES[p], x_from * 2 + h_from]
        return net.copy(block, block, device)

    def to_other_core(x_from, h_from):
        at = x_from * 2 + h_from
        twins.append(net.copy(every.at[:, at], twin.at[:, at], to_twin))

    for one in loads:
        one.wait()
    back[0:5] = tn(
        w_zero[...].reshape(5 * local, 5 * C), grads[0:5].reshape(5 * local, edges)
    ).astype(BF16).reshape(5, 8, local, edges)

    near_r[0].wait_recv()
    over_r = [forward(0, xl, h, to_xr)]
    near_l[1].wait_recv()
    over_l = [forward(1, xr, h, to_xl)]
    cross_r, cross_l = [], []
    cross[0].wait_recv()
    cross_r.append(forward(0, x, 1 - h, to_xr))
    cross_l.append(forward(0, x, 1 - h, to_xl))

    for w, start, blocks in ((w_one, 5, 4), (w_two, 13, 3)):
        plus = grads[start : start + blocks].reshape(blocks * local, edges)
        minus = grads[start + blocks : start + 2 * blocks].reshape(blocks * local, edges)
        both = jnp.concatenate([plus, minus], axis=1)
        turned = jnp.concatenate([minus, -plus], axis=1)
        size = blocks * C
        out = tn(w[0].reshape(blocks * local, size), both) + tn(
            w[1].reshape(blocks * local, size), turned
        )
        back[start : start + blocks] = (
            out[:, :edges].astype(BF16).reshape(blocks, 8, local, edges)
        )
        back[start + blocks : start + 2 * blocks] = (
            out[:, edges:].astype(BF16).reshape(blocks, 8, local, edges)
        )

    for one in asked:
        one.wait_recv()
    square_sum = square[...]
    for i in range(7):
        square_sum = square_sum + squares[i]
    inverse_both = lax.rsqrt(square_sum / (25 * C) + EPSILON)
    inverse, inverse_a = inverse_both[0:1, :], inverse_both[1:2, :]
    for j in range(19):
        scaled[j] = (grads[j].astype(F32) * inverse).astype(BF16)
    scaled_copy = net.copy(scaled, scaled_twin, to_twin)

    cross[1].wait_recv()
    cross_r.append(forward(1, x, 1 - h, to_xr))
    cross_l.append(forward(1, x, 1 - h, to_xl))
    to_other_core(x, 1 - h)
    near_r[1].wait_recv()
    to_other_core(xl, h)
    near_l[0].wait_recv()
    to_other_core(xr, h)
    over_r[0].wait_recv()
    over_l[0].wait_recv()
    to_other_core(xo, h)
    cross_r[0].wait_recv()
    over_r.append(forward(0, xl, 1 - h, to_xr))
    cross_l[1].wait_recv()
    over_l.append(forward(1, xr, 1 - h, to_xl))

    half = (1 - h, h)
    steps = []
    for q in (0, 1):
        steps.append(
            [
                net.copy(back.at[PIECES[0], xo * 2 + half[q]], relay_left.at[q], to_xr),
                net.copy(back.at[PIECES[1], xo * 2 + half[q]], relay_right.at[q], to_xl),
                net.copy(
                    back.at[PIECES[1], xr * 2 + half[q]], from_left.at[q, PIECES[1]], to_xr
                ),
                net.copy(
                    back.at[PIECES[0], xl * 2 + half[q]], from_right.at[q, PIECES[0]], to_xl
                ),
            ]
        )

    cross_r[1].wait_recv()
    to_other_core(xl, 1 - h)
    cross_l[0].wait_recv()
    to_other_core(xr, 1 - h)
    over_r[1].wait_recv()
    over_l[1].wait_recv()
    to_other_core(xo, 1 - h)

    def spread_flat(buffer, lane):
        def rows(start, blocks):
            return buffer[start : start + blocks].reshape(blocks * C, edges)

        flat_zero[:, lane * edges : (lane + 1) * edges] = rows(0, 5)
        for flat, start, blocks in ((flat_one, 5, 4), (flat_two, 13, 3)):
            for i in (0, 1):
                at = (2 * lane + i) * edges
                flat[:, at : at + edges] = rows(start + i * blocks, blocks)

    spread_flat(every, 0)

    def right_side(buffer, lane):
        wide = 5 * local
        right_zero[0:wide, lane * edges : (lane + 1) * edges] = buffer[0:5].reshape(wide, edges)
        for right, start, blocks in ((right_one, 5, 4), (right_two, 13, 3)):
            rows = blocks * local
            plus = buffer[start : start + blocks].reshape(rows, edges)
            minus = buffer[start + blocks : start + 2 * blocks].reshape(rows, edges)
            at = 2 * lane * edges
            right[0:rows, at : at + edges] = plus
            right[0:rows, at + edges : at + 2 * edges] = minus
            right[rows : 2 * rows, at : at + edges] = minus
            right[rows : 2 * rows, at + edges : at + 2 * edges] = -plus

    right_zero[...] = jnp.zeros_like(right_zero)
    right_side(scaled, 0)
    scaled_copy.wait_recv()
    right_side(scaled_twin, 1)
    for one in twins:
        one.wait_recv()
    spread_flat(twin, 1)
    for flat, sel, rows in (
        (flat_zero, sel_zero, 80),
        (flat_one, sel_one, 64),
        (flat_two, sel_two, 48),
    ):
        for i in range(16):
            begin = pl.multiple_of((2 * i + core) * rows, 16)
            sel[i * rows : (i + 1) * rows, :] = flat[pl.ds(begin, rows), :]
    at = 0
    for sel, right, rows, tiles in (
        (sel_zero, right_zero, 80, 3),
        (sel_one, right_one, 64, 4),
        (sel_two, right_two, 48, 3),
    ):
        for quarter in range(4):
            out = nt(sel[quarter * 4 * rows : (quarter + 1) * 4 * rows, :], right[...])
            out = out.astype(BF16).reshape(4, rows, 128 * tiles)
            for tile in range(tiles):
                part[quarter, :, at + tile * rows : at + (tile + 1) * rows, :] = out[
                    :, :, 128 * tile : 128 * (tile + 1)
                ]
        at += rows * tiles

    climbs = {}

    def climb(o):
        to = lax.rem(z + o, 4)
        climbs[o] = [
            net.copy(part.at[yo, to, HALVES[0]], pass_left.at[o], to_yr),
            net.copy(part.at[yo, to, HALVES[1]], pass_right.at[o], to_yl),
            net.copy(part.at[yr, to, HALVES[1]], up_left.at[o, HALVES[1]], to_yr),
            net.copy(part.at[yl, to, HALVES[0]], up_right.at[o, HALVES[0]], to_yl),
        ]

    def added(a, b):
        return (a.astype(F32) + b.astype(F32)).astype(BF16)

    def climb_on(o):
        to = lax.rem(z + o, 4)
        climbs[o][0].wait_recv()
        part[yr, to, HALVES[0]] = added(part[yr, to, HALVES[0]], pass_left[o])
        climbs[o].append(
            net.copy(part.at[yr, to, HALVES[0]], up_left.at[o, HALVES[0]], to_yr)
        )
        climbs[o][1].wait_recv()
        part[yl, to, HALVES[1]] = added(part[yl, to, HALVES[1]], pass_right[o])
        climbs[o].append(
            net.copy(part.at[yl, to, HALVES[1]], up_right.at[o, HALVES[1]], to_yl)
        )

    lines = []

    def climbed(o):
        to = lax.rem(z + o, 4)
        for one in climbs[o][2:]:
            one.wait_recv()
        total = part[y, to].astype(F32) + up_left[o].astype(F32) + up_right[o].astype(F32)
        if o:
            to_line[o - 1] = total.astype(BF16)
            lines.append(net.copy(to_line.at[o - 1], line.at[o - 1], line_peers[o]))
        else:
            kept[...] = total

    def step_on(q):
        steps[q][0].wait_recv()
        for j in range(10):
            back[j, xr * 2 + half[q]] = added(back[j, xr * 2 + half[q]], relay_left[q, j])
        steps[q].append(
            net.copy(back.at[PIECES[0], xr * 2 + half[q]], from_left.at[q, PIECES[0]], to_xr)
        )
        steps[q][1].wait_recv()
        for j in range(10, 19):
            back[j, xl * 2 + half[q]] = added(
                back[j, xl * 2 + half[q]], relay_right[q, j - 10]
            )
        steps[q].append(
            net.copy(back.at[PIECES[1], xl * 2 + half[q]], from_right.at[q, PIECES[1]], to_xl)
        )

    def stepped(q):
        for one in steps[q][2:]:
            one.wait_recv()

    def own_sum(q, j):
        return (
            back[j, x * 2 + half[q]].astype(F32)
            + from_left[q, j].astype(F32)
            + from_right[q, j].astype(F32)
        )

    climb(1)
    climb(2)
    step_on(0)

    mixed[0:5] = nn(w_zero[...].reshape(5 * local, 5 * C), flat_zero[:, 0:edges]).reshape(
        5, local, edges
    )
    for w, flat, start, blocks in ((w_one, flat_one, 5, 4), (w_two, flat_two, 13, 3)):
        size = blocks * C
        both = flat[:, 0 : 2 * edges]
        real = nn(w[0].reshape(blocks * local, size), both)
        imag = nn(w[1].reshape(blocks * local, size), both)
        mixed[start : start + blocks] = (real[:, :edges] - imag[:, edges:]).reshape(
            blocks, local, edges
        )
        mixed[start + blocks : start + 2 * blocks] = (
            real[:, edges:] + imag[:, :edges]
        ).reshape(blocks, local, edges)
    total = jnp.zeros((1, edges), F32)
    for j in range(19):
        total = total + jnp.sum(mixed[j] * grads[j].astype(F32), axis=0, keepdims=True)
    tally[...] = jnp.broadcast_to(total, tally.shape)
    counted = [net.copy(tally, tallies.at[i], d) for i, d in enumerate(chan_peers)]

    step_on(1)
    climb_on(1)
    climb(3)
    stepped(0)
    for j in range(19):
        to_far[j] = own_sum(0, j).astype(BF16)
    far_copy = net.copy(to_far, far, to_far_half)
    climb_on(2)
    climb(0)

    scale = weight[...] * inverse
    for j in range(19):
        mixed[j] = mixed[j] * scale
    for l in range(5):
        for k in range(l * l, (l + 1) * (l + 1)):
            message[k] = rotate_out(rot, mixed, k, l).astype(BF16)
    update[...] = (
        nt(message[...].reshape(count, edges), arrive).reshape(25, local, atoms).astype(BF16)
    )

    climbed(1)
    climb_on(3)
    climbed(2)
    climb_on(0)
    stepped(1)
    for j in range(19):
        mixed[j] = own_sum(1, j)
    climbed(3)

    for one in counted:
        one.wait_recv()
    tally_sum = tally[...]
    for i in range(7):
        tally_sum = tally_sum + tallies[i]
    far_copy.wait_recv()
    for j in range(19):
        mixed[j] = mixed[j] + far[j].astype(F32)
    for l in range(5):
        for k in range(l * l, (l + 1) * (l + 1)):
            message[k] = rotate_out(rot, mixed, k, l).astype(BF16)
    flat = message[...].reshape(count, edges)
    leaving[...] = nt(near, flat).astype(BF16)

    def exact(left, right, dims):
        return lax.dot_general(
            left, right, (dims, ((), ())),
            precision=lax.Precision.HIGHEST, preferred_element_type=F32,
        )

    tally_out[...] = exact(
        tally_sum, hot(source[...], 128, atoms).astype(F32), ((1,), (1,))
    )
    halo = [
        net.copy(leaving.at[16:32], returned.at[0:16], to_ahead),
        net.copy(leaving.at[0:16], returned.at[16:32], to_behind),
        net.copy(tally_out, tally_in.at[0], to_ahead),
        net.copy(tally_out, tally_in.at[1], to_behind),
    ]
    own[...] = nt(flat, here).reshape(25, local, atoms)
    tally_a = exact(tally_sum, here.astype(F32), ((1,), (1,)))
    climbed(0)
    for one in halo:
        one.wait_recv()
    settled[...] = tn(returned[...], face_hot).reshape(25, local, atoms)
    wide = lax.broadcasted_iota(jnp.int32, (128, atoms), 1)
    for i, column in ((0, face_left), (1, face_right)):
        tally_a = tally_a + exact(
            tally_in[i], jnp.where(wide == column[...], 1.0, 0.0), ((1,), (0,))
        )
    factor = inverse_a * inverse_a * inverse_a * tally_a[0:1, :] / (25 * C)
    for l in range(5):
        gain = gain_t[:, l : l + 1] * inverse_a
        for k in range(l * l, (l + 1) * (l + 1)):
            grad_embed[k] = (
                (own[k] + settled[k]) * gain - embed[k].astype(F32) * factor
            ).astype(BF16)
    for one in lines:
        one.wait_recv()
    total = kept[...]
    for i in range(3):
        total = total + line[i].astype(F32)
    sums[...] = total
    net.finish()


def shards(
    embed, gain, w_zero, w_one, w_two, rot_table, face_atoms, edge_source, edge_target,
    rot_index, edge_weight, cotangent,
):
    atoms = embed.shape[2]
    local = embed.shape[1]
    edges = edge_source.shape[0]
    row = lambda a: a.reshape(1, edges)
    column = lambda a: a.reshape(-1, 1)
    lost = lambda n: jnp.full((n,), -1, jnp.int32)
    face_left = column(jnp.concatenate([lost(16), face_atoms[:16], lost(96)]))
    face_right = column(jnp.concatenate([face_atoms[16:], lost(112)]))
    vmem = pl.BlockSpec(memory_space=pltpu.VMEM)
    hbm = pl.BlockSpec(memory_space=pl.ANY)
    block = (19, local, edges)
    scratch = [
        (w_zero.shape, BF16),
        (w_one.shape, BF16),
        (w_two.shape, BF16),
        ((32, 25 * local), BF16),
        ((32, 25 * local), BF16),
        ((19, 25, edges), F32),
        ((25, local, edges), F32),
        (block, BF16),
        (block, BF16),
        ((8, edges), F32),
        ((7, 8, edges), F32),
        ((19, 8, local, edges), BF16),
        ((19, 8, local, edges), BF16),
        ((19, 8, local, edges), BF16),
        ((2, 10, local, edges), BF16),
        ((2, 9, local, edges), BF16),
        ((2, 19, local, edges), BF16),
        ((2, 19, local, edges), BF16),
        (block, BF16),
        (block, BF16),
        (block, BF16),
        (block, BF16),
        ((5 * C, 2 * edges), BF16),
        ((4 * C, 4 * edges), BF16),
        ((3 * C, 4 * edges), BF16),
        ((1280, 2 * edges), BF16),
        ((1024, 4 * edges), BF16),
        ((768, 4 * edges), BF16),
        ((384, 2 * edges), BF16),
        ((512, 4 * edges), BF16),
        ((384, 4 * edges), BF16),
        ((4, 4, 640, 128), BF16),
        ((4, 320, 128), BF16),
        ((4, 320, 128), BF16),
        ((4, 640, 128), BF16),
        ((4, 640, 128), BF16),
        ((3, 640, 128), BF16),
        ((3, 640, 128), BF16),
        ((640, 128), F32),
        (block, F32),
        ((25, local, edges), BF16),
        ((8, edges), F32),
        ((7, 8, edges), F32),
        ((25, local, atoms), F32),
        ((32, 25 * local), BF16),
        ((32, 25 * local), BF16),
        ((8, 128), F32),
        ((2, 8, 128), F32),
        ((25, local, atoms), F32),
    ]
    update, grad_embed, sums = pl.pallas_call(
        layer_kernel,
        name="layer",
        out_shape=[
            jax.ShapeDtypeStruct((25, local, atoms), BF16),
            jax.ShapeDtypeStruct((25, local, atoms), BF16),
            jax.ShapeDtypeStruct((640, 128), F32),
        ],
        in_specs=[vmem] * 11 + [hbm] * 3,
        out_specs=[vmem] * 3,
        scratch_shapes=[pltpu.VMEM(s, t) for s, t in scratch]
        + [
            pltpu.SemaphoreType.DMA((COPIES,)),
            pltpu.SemaphoreType.DMA((COPIES,)),
            pltpu.SemaphoreType.DMA((3,)),
        ],
        compiler_params=pltpu.CompilerParams(
            vmem_limit_bytes=VMEM_LIMIT, collective_id=0, has_side_effects=True
        ),
    )(
        embed, cotangent, gain.T, rot_table, column(face_atoms), face_left, face_right,
        row(edge_source), row(edge_target), row(rot_index), row(edge_weight),
        w_zero, w_one, w_two,
    )

    def owned(first, rows, tiles, width):
        piece = sums[first : first + rows * tiles].reshape(tiles, rows, 128)
        return piece.transpose(0, 2, 1).reshape(tiles * 128, rows)[:width]

    grad_zero = owned(0, 80, 3, 5 * local).reshape(5, local, 80)
    grad_one = owned(240, 64, 4, 8 * local).reshape(2, 4, local, 64)
    grad_two = owned(496, 48, 3, 6 * local).reshape(2, 3, local, 48)
    return (update, grad_embed, grad_zero, grad_one, grad_two)


def solution(mesh):
    torus = Mesh(mesh.devices.reshape(4, 4, 2, 4, 2), ("y", "z", "core", "x", "zh"))
    return jax.shard_map(
        shards,
        mesh=torus,
        in_specs=(
            P(None, CHAN, GRAPH),
            P(None, CHAN),
            P(None, CHAN, None),
            P(None, None, CHAN, None),
            P(None, None, CHAN, None),
            P(),
            P(GRAPH),
            P(GRAPH),
            P(GRAPH),
            P(GRAPH),
            P(GRAPH),
            P(None, CHAN, GRAPH),
        ),
        out_specs=(
            P(None, CHAN, GRAPH),
            P(None, CHAN, GRAPH),
            P(None, CHAN, GRAPH),
            P(None, None, CHAN, GRAPH),
            P(None, None, CHAN, GRAPH),
        ),
        check_vma=False,
    )
```

time: 896 us -> 105 us (0.12)
  the two profiles are of different devices: /device:TPU:1 before, /device:TPU:64 now
where the time goes in v1:
time: 105 us
  Pallas kernels  90.1 us (86%)
  local copies, waits for them, and re-layouts  13.9 us (13%)
    pallas_call x1, Pallas kernels, shards(): pl.pallas_call(layer_kernel, name='layer', out_shape=[jax.ShapeDtypeStruc...  90.1 us
    unnamed x10, local copies, waits for them, and re-layouts  5.67 us
    reshape x3, local copies, waits for them, and re-layouts, shards(): column = lambda a: a.reshape(-1, 1)  2.82 us
    slice x3, local copies, waits for them, and re-layouts, owned(): piece = sums[first:first + rows * tiles].reshape(tiles, rows, 128)  2.76 us

profile of v1, /device:TPU:64, one launch (start us, length us, event | category | flops | bytes accessed | tf_op | source)
XLA Modules:
  0.0 104.8 jit_solution(11961406119986129447)
XLA Ops:
  0.6 0.8 fusion
  1.4 0.1 add_bitcast_fusion
  1.5 1.3 %copy.35.face = s32[32,1]{1,0:T(8,128)} copy(s32[32,1]{0,1:T(1,128)} %bitcast.39) | data formatting | bytes 256 | tf_op jit(solution)/shard_map/reshape | solution.py:520
  2.9 1.4 %copy.33 = f32[5,64]{0,1:T(8,128)} copy(f32[5,64]{1,0:T(8,128)} %param.13) | data formatting | bytes 2560 | tf_op args[1]
  4.2 0.7 copy.36.face_left
  5.0 0.7 copy.37.face_right
  5.7 2.1 %copy.34.rot_table = f32[19,25,256]{2,1,0:T(8,128)} copy(f32[19,25,256]{2,0,1:T(8,128)} %param.17) | data formatting | bytes 972800 | tf_op args[5]
  7.8 90.1 %layer.1 = (bf16[25,64,128]{2,1,0:T(8,128)(2,1)}, bf16[25,64,128]{2,1,0:T(8,128)(2,1)}, f32[640,128]{1,0:T(8,128)}) custom-call(bf16[25,64,128]{2,1,0:T(8,128)(2,1)} %embed.1, bf16[25,64,128]{2,1,0:T(8,128)(2,1)} %cotangent.1, f32[64,5]{1,0:T(8,128)} %bitcast.38, f32[19,25,256]{2,1,0:T(8,128)} %copy.34.rot_table, s32[32,1]{1,0:T(8,128)} %copy.35.face, ...), custom_call_target="tpu_custom_call" | custom-call | tf_op jit(solution)/shard_map/layer/pallas_call | solution.py:578
  97.9 0.0 copy-start.1
  98.0 0.9 slice.23
  98.9 0.0 copy-start
  99.0 0.1 reshape_reshape.7
  99.1 0.7 copy.42
  99.8 0.9 slice.20
  100.7 0.9 slice.22
  101.6 0.1 copy.38
  101.7 0.8 copy.39
  102.5 0.8 copy.40
  103.3 0.0 copy-done.1
  103.3 0.8 copy.50
  104.1 0.0 copy-done
  104.1 0.8 copy.51
  (4 shorter events, 0.1 us)
Async XLA Ops:
  97.9 5.4 %copy-start.1 = (bf16[25,64,128]{2,1,0:T(8,128)(2,1)S(1)}, bf16[25,64,128]{2,1,0:T(8,128)(2,1)}, u32[]{:S(2)}) copy-start(bf16[25,64,128]{2,1,0:T(8,128)(2,1)} %get-tuple-element.30) | copy-start | bytes 1228804
  98.9 5.1 %copy-start = (bf16[25,64,128]{2,1,0:T(8,128)(2,1)S(1)}, bf16[25,64,128]{2,1,0:T(8,128)(2,1)}, u32[]{:S(2)}) copy-start(bf16[25,64,128]{2,1,0:T(8,128)(2,1)} %get-tuple-element.31) | copy-start | bytes 1228804

commit v2 on v1

v2 whole, which is shorter than its diff:
```python
import jax
import jax.numpy as jnp
from jax import lax
from jax.experimental import pallas as pl
from jax.experimental.pallas import tpu as pltpu
from jax.sharding import Mesh
from jax.sharding import PartitionSpec as P

C = 512
EPSILON = 1e-06
CHAN = ("x", "zh")
GRAPH = ("y", "z", "core")
DEGREE = (0, 1, 2, 3, 4, 1, 2, 3, 4, 1, 2, 3, 4, 2, 3, 4, 2, 3, 4)
ROWS = tuple(tuple(j for j in range(19) if DEGREE[j] == l) for l in range(5))
F32 = jnp.float32
BF16 = jnp.bfloat16
VMEM_LIMIT = 60 * 1024 * 1024
MESH = pl.DeviceIdType.MESH
PIECES = (slice(5, 13), slice(0, 5), slice(13, 19))
HALF = (slice(0, 10), slice(10, 19))
UNIT = (64, 80, 48)
TILES = (4, 3, 3)
SPLIT = (128, 128, 80)


def nt(left, right):
    return lax.dot_general(left, right, (((1,), (1,)), ((), ())), preferred_element_type=F32)


def tn(left, right):
    return lax.dot_general(left, right, (((0,), (0,)), ((), ())), preferred_element_type=F32)


def nn(left, right):
    return jnp.dot(left, right, preferred_element_type=F32)


def hot(index_row, rows, first=0):
    edges = index_row.shape[1]
    row = lax.broadcasted_iota(jnp.int32, (rows, edges), 0) + first
    return jnp.where(row == index_row, 1.0, 0.0).astype(BF16)


def rotate_in(rot, values, j):
    l = DEGREE[j]
    total = None
    for k in range(l * l, (l + 1) * (l + 1)):
        term = rot[k, j : j + 1, :] * values[k]
        total = term if total is None else total + term
    return total


def rotate_out(rot, values, k, l):
    total = None
    for j in ROWS[l]:
        term = rot[k, j : j + 1, :] * values[j]
        total = term if total is None else total + term
    return total


class Net:
    def __init__(self, send, recv):
        self.send, self.recv, self.started = send, recv, []

    def copy(self, source, landing, device):
        at = len(self.started)
        assert at < COPIES
        one = pltpu.make_async_remote_copy(
            src_ref=source,
            dst_ref=landing,
            send_sem=self.send.at[at],
            recv_sem=self.recv.at[at],
            device_id=device,
            device_id_type=MESH,
        )
        one.start()
        self.started.append(one)
        return one

    def finish(self):
        for one in self.started:
            one.wait_send()


COPIES = 92


def layer_kernel(
    embed, cotangent, gain, rot_table, face,
    source, target, spin, weight, w_zero_hbm, w_one_hbm, w_two_hbm,
    update, grad_embed, sum_zero, sum_one, sum_two,
    w_zero, w_one, w_two, corner, gain_t, faces, halo_t, rot, values, grads, mine, square, squares, every, twin,
    back, relay_left, relay_right, from_left, from_right, to_far, far,
    scaled, scaled_twin, flat_zero, flat_one, flat_two, sel_zero, sel_one, sel_two,
    right_zero, right_one, right_two,
    part_one, pass_left_one, pass_right_one, up_left_one, up_right_one, to_line_one, line_one,
    kept_one,
    part_zero, pass_left_zero, pass_right_zero, up_left_zero, up_right_zero, to_line_zero,
    line_zero, kept_zero,
    part_two, pass_left_two, pass_right_two, up_left_two, up_right_two, to_line_two, line_two,
    kept_two,
    mixed, message, tally, tallies, own, leaving, returned,
    tally_out, tally_in, settled, send, recv, load,
):
    x, h = lax.axis_index("x"), lax.axis_index("zh")
    y, z, core = lax.axis_index("y"), lax.axis_index("z"), lax.axis_index("core")
    xr, xl, xo = lax.rem(x + 1, 4), lax.rem(x + 3, 4), lax.rem(x + 2, 4)
    yr, yl, yo = lax.rem(y + 1, 4), lax.rem(y + 3, 4), lax.rem(y + 2, 4)
    me = y * 8 + z * 2 + core
    ahead, behind = lax.rem(me + 1, 32), lax.rem(me + 31, 32)

    def graph_at(g):
        return {"y": g // 8, "z": lax.rem(g // 2, 4), "core": lax.rem(g, 2)}

    to_xr, to_xl = {"x": xr}, {"x": xl}
    to_yr, to_yl = {"y": yr}, {"y": yl}
    to_far_half = {"zh": 1 - h}
    to_twin = {"core": 1 - core}
    to_ahead, to_behind = graph_at(ahead), graph_at(behind)
    chan_peers = [
        {"x": lax.rem(x + dx, 4), "zh": lax.rem(h + dh, 2)}
        for dx in range(4)
        for dh in range(2)
        if dx or dh
    ]
    line_peers = [None] + [{"z": lax.rem(z + o, 4)} for o in (1, 2, 3)]
    chan = x * 2 + h

    local = embed.shape[1]
    atoms = embed.shape[2]
    edges = source.shape[1]
    count = 25 * local
    net = Net(send, recv)

    loads = [
        pltpu.make_async_copy(a, b, load.at[i])
        for i, (a, b) in enumerate(
            ((w_zero_hbm, w_zero), (w_one_hbm, w_one), (w_two_hbm, w_two))
        )
    ]
    for one in loads:
        one.start()

    barrier = pltpu.get_barrier_semaphore()
    partners = chan_peers + line_peers[1:] + [to_yr, to_yl, to_ahead, to_behind]
    for device in partners:
        pl.semaphore_signal(barrier, inc=1, device_id=device, device_id_type=MESH)

    corner[...] = jnp.zeros_like(corner)
    corner[0:1, 0:32] = face[...].astype(F32)
    face_col = jnp.broadcast_to(corner[0:1, :], (128, 128)).T[0:32].astype(jnp.int32)
    face_row = lax.broadcasted_iota(jnp.int32, (32, atoms), 1)
    face_hot = jnp.where(face_row == face_col, 1.0, 0.0).astype(BF16)
    flat_embed = embed[...].reshape(count, atoms)
    faces[...] = nt(face_hot, flat_embed).astype(BF16)
    pl.semaphore_wait(barrier, len(partners))
    halo = [
        net.copy(faces.at[16:32], halo_t.at[0:16], to_ahead),
        net.copy(faces.at[0:16], halo_t.at[16:32], to_behind),
    ]

    corner[0:5, 0:local] = gain[...]
    gain_t[...] = corner[...].T
    turn = hot(spin[...], rot_table.shape[2])
    for k in range(25):
        line_k = rot_table[k]
        high = line_k.astype(BF16)
        low = (line_k - high.astype(F32)).astype(BF16)
        rot[k] = nn(high, turn) + nn(low, turn)
    total_a = jnp.zeros((1, atoms), F32)
    for k in range(25):
        one = embed[k].astype(F32)
        total_a = total_a + jnp.sum(one * one, axis=0, keepdims=True)
    here = hot(source[...], atoms)
    near = hot(source[...], 32, atoms)

    for one in halo:
        one.wait_recv()
    values[...] = (nn(flat_embed, here) + tn(halo_t[...], near)).reshape(25, local, edges)
    for j in range(19):
        l = DEGREE[j]
        mine[j] = (rotate_in(rot, values, j) * gain_t[0:local, l : l + 1]).astype(BF16)
    cross, near_r, near_l = [], [], []
    for p in range(3):
        here_at = mine.at[PIECES[p]]
        there_at = every.at[PIECES[p], x, h]
        cross.append(net.copy(here_at, there_at, to_far_half))
        near_r.append(net.copy(here_at, there_at, to_xr))
        near_l.append(net.copy(here_at, there_at, to_xl))
    total_e = jnp.zeros((1, edges), F32)
    for k in range(25):
        one = values[k]
        total_e = total_e + jnp.sum(one * one, axis=0, keepdims=True)
    square[...] = jnp.concatenate([total_e, total_a, jnp.zeros((6, edges), F32)], axis=0)
    asked = [net.copy(square, squares.at[i], d) for i, d in enumerate(chan_peers)]
    for j in range(19):
        every[j, x, h] = mine[j]

    arrive = hot(target[...], atoms)
    values[...] = nn(cotangent[...].reshape(count, atoms), arrive).reshape(25, local, edges)
    for j in range(19):
        grads[j] = (rotate_in(rot, values, j) * weight[...]).astype(BF16)

    for one in loads:
        one.wait()
    back[0:5] = tn(
        w_zero[...].reshape(5 * local, 5 * C), grads[0:5].reshape(5 * local, edges)
    ).astype(BF16).reshape(5, 4, 2, local, edges)
    for w, start, blocks in ((w_one, 5, 4), (w_two, 13, 3)):
        plus = grads[start : start + blocks].reshape(blocks * local, edges)
        minus = grads[start + blocks : start + 2 * blocks].reshape(blocks * local, edges)
        both = jnp.concatenate([plus, minus], axis=1)
        turned = jnp.concatenate([minus, -plus], axis=1)
        size = blocks * C
        out = tn(w[0].reshape(blocks * local, size), both) + tn(
            w[1].reshape(blocks * local, size), turned
        )
        back[start : start + blocks] = (
            out[:, :edges].astype(BF16).reshape(blocks, 4, 2, local, edges)
        )
        back[start + blocks : start + 2 * blocks] = (
            out[:, edges:].astype(BF16).reshape(blocks, 4, 2, local, edges)
        )

    def added(a, b):
        return (a.astype(F32) + b.astype(F32)).astype(BF16)

    half = (1 - h, h)
    steps = [[], []]

    def step(q):
        to = half[q]
        steps[q] = [
            net.copy(back.at[HALF[0], xo, to], relay_left.at[q], to_xr),
            net.copy(back.at[HALF[1], xo, to], relay_right.at[q], to_xl),
            net.copy(back.at[HALF[1], xr, to], from_left.at[q, HALF[1]], to_xr),
            net.copy(back.at[HALF[0], xl, to], from_right.at[q, HALF[0]], to_xl),
        ]

    def step_on(q):
        to = half[q]
        steps[q][0].wait_recv()
        for j in range(10):
            back[j, xr, to] = added(back[j, xr, to], relay_left[q, j])
        steps[q].append(
            net.copy(back.at[HALF[0], xr, to], from_left.at[q, HALF[0]], to_xr)
        )
        steps[q][1].wait_recv()
        for j in range(10, 19):
            back[j, xl, to] = added(back[j, xl, to], relay_right[q, j - 10])
        steps[q].append(
            net.copy(back.at[HALF[1], xl, to], from_right.at[q, HALF[1]], to_xl)
        )

    def own_sum(q, j):
        return (
            back[j, x, half[q]].astype(F32)
            + from_left[q, j].astype(F32)
            + from_right[q, j].astype(F32)
        )

    fars = []

    def send_far(i):
        for at in ((4, 3), (2, 5))[i]:
            steps[0][at].wait_recv()
        for j in range(19)[HALF[i]]:
            to_far[j] = own_sum(0, j).astype(BF16)
        fars.append(net.copy(to_far.at[HALF[i]], far.at[HALF[i]], to_far_half))

    def forward(p, x_from, h_from, device):
        block = every.at[PIECES[p], x_from, h_from]
        return net.copy(block, block, device)

    over_own, over_cross, cross_r, cross_l = {}, {}, {}, {}
    twins = [[], [], []]

    def to_twin_core(p, h_from):
        block = every.at[PIECES[p], :, h_from]
        twins[p].append(net.copy(block, twin.at[PIECES[p], :, h_from], to_twin))

    step(0)
    near_r[0].wait_recv()
    over_own[0] = forward(0, xl, h, to_xr)
    near_l[1].wait_recv()
    over_own[1] = forward(1, xr, h, to_xl)
    near_l[2].wait_recv()
    over_own[2] = forward(2, xr, h, to_xl)
    cross[0].wait_recv()
    cross_r[0] = forward(0, x, 1 - h, to_xr)
    cross_l[0] = forward(0, x, 1 - h, to_xl)
    step_on(0)
    cross[1].wait_recv()
    cross_r[1] = forward(1, x, 1 - h, to_xr)
    cross_l[1] = forward(1, x, 1 - h, to_xl)

    for one in asked:
        one.wait_recv()
    square_sum = square[...]
    for i in range(7):
        square_sum = square_sum + squares[i]
    inverse_both = lax.rsqrt(square_sum / (25 * C) + EPSILON)
    inverse, inverse_a = inverse_both[0:1, :], inverse_both[1:2, :]
    for j in range(19):
        scaled[j] = (grads[j].astype(F32) * inverse).astype(BF16)
    scaled_copy = net.copy(scaled, scaled_twin, to_twin)

    def right_side(buffer, lane):
        wide = 5 * local
        right_zero[0:wide, lane * edges : (lane + 1) * edges] = buffer[0:5].reshape(wide, edges)
        for right, start, blocks in ((right_one, 5, 4), (right_two, 13, 3)):
            rows = blocks * local
            plus = buffer[start : start + blocks].reshape(rows, edges)
            minus = buffer[start + blocks : start + 2 * blocks].reshape(rows, edges)
            at = 2 * lane * edges
            right[0:rows, at : at + edges] = plus
            right[0:rows, at + edges : at + 2 * edges] = minus
            right[rows : 2 * rows, at : at + edges] = minus
            right[rows : 2 * rows, at + edges : at + 2 * edges] = -plus

    right_zero[...] = jnp.zeros_like(right_zero)
    right_side(scaled, 0)

    cross[2].wait_recv()
    cross_r[2] = forward(2, x, 1 - h, to_xr)
    cross_l[2] = forward(2, x, 1 - h, to_xl)
    near_l[0].wait_recv()
    over_own[0].wait_recv()
    to_twin_core(0, h)
    for p in (1, 2):
        near_r[p].wait_recv()
        over_own[p].wait_recv()
        to_twin_core(p, h)
    cross_l[0].wait_recv()
    over_cross[0] = forward(0, xr, 1 - h, to_xl)
    send_far(0)
    cross_r[1].wait_recv()
    over_cross[1] = forward(1, xl, 1 - h, to_xr)
    send_far(1)
    cross_r[2].wait_recv()
    over_cross[2] = forward(2, xl, 1 - h, to_xr)
    step(1)

    flats = (flat_one, flat_zero, flat_two)
    sels = (sel_one, sel_zero, sel_two)
    rights = (right_one, right_zero, right_two)
    parts = (part_one, part_zero, part_two)
    pass_left = (pass_left_one, pass_left_zero, pass_left_two)
    pass_right = (pass_right_one, pass_right_zero, pass_right_two)
    up_left = (up_left_one, up_left_zero, up_left_two)
    up_right = (up_right_one, up_right_zero, up_right_two)
    to_line = (to_line_one, to_line_zero, to_line_two)
    line = (line_one, line_zero, line_two)
    kept = (kept_one, kept_zero, kept_two)

    def spread_flat(buffer, lane, p):
        start, blocks, runs = ((5, 4, 2), (0, 5, 1), (13, 3, 2))[p]
        for i in range(runs):
            at = (runs * lane + i) * edges
            flats[p][:, at : at + edges] = buffer[
                start + i * blocks : start + (i + 1) * blocks
            ].reshape(blocks * C, edges)

    climbs, lines = [None] * 3, []

    def halves(p):
        return slice(0, SPLIT[p]), slice(SPLIT[p], UNIT[p] * TILES[p])

    def climb(p):
        for one in twins[p]:
            one.wait_recv()
        spread_flat(twin, 1, p)
        rows, tiles = UNIT[p], TILES[p]
        for i in range(16):
            begin = pl.multiple_of((2 * i + core) * rows, 16)
            sels[p][i * rows : (i + 1) * rows, :] = flats[p][pl.ds(begin, rows), :]
        for quarter in range(4):
            out = nt(
                sels[p][quarter * 4 * rows : (quarter + 1) * 4 * rows, :], rights[p][...]
            )
            out = out.astype(BF16).reshape(4, rows, 128 * tiles)
            for tile in range(tiles):
                parts[p][quarter, :, tile * rows : (tile + 1) * rows, :] = out[
                    :, :, 128 * tile : 128 * (tile + 1)
                ]
        a, b = halves(p)
        climbs[p] = [
            net.copy(parts[p].at[yo, :, a], pass_left[p], to_yr),
            net.copy(parts[p].at[yo, :, b], pass_right[p], to_yl),
            net.copy(parts[p].at[yr, :, b], up_left[p].at[:, b], to_yr),
            net.copy(parts[p].at[yl, :, a], up_right[p].at[:, a], to_yl),
        ]

    def climb_on(p):
        a, b = halves(p)
        climbs[p][0].wait_recv()
        parts[p][yr, :, a] = added(parts[p][yr, :, a], pass_left[p][...])
        climbs[p].append(net.copy(parts[p].at[yr, :, a], up_left[p].at[:, a], to_yr))
        climbs[p][1].wait_recv()
        parts[p][yl, :, b] = added(parts[p][yl, :, b], pass_right[p][...])
        climbs[p].append(net.copy(parts[p].at[yl, :, b], up_right[p].at[:, b], to_yl))

    def climbed(p):
        for one in climbs[p][2:]:
            one.wait_recv()
        for o in (2, 3, 1, 0):
            to = lax.rem(z + o, 4)
            total = (
                parts[p][y, to].astype(F32)
                + up_left[p][to].astype(F32)
                + up_right[p][to].astype(F32)
            )
            if o:
                to_line[p][o - 1] = total.astype(BF16)
                lines.append(
                    net.copy(to_line[p].at[o - 1], line[p].at[o - 1], line_peers[o])
                )
            else:
                kept[p][...] = total

    cross_r[0].wait_recv()
    over_cross[0].wait_recv()
    to_twin_core(0, 1 - h)
    spread_flat(every, 0, 0)
    scaled_copy.wait_recv()
    right_side(scaled_twin, 1)
    cross_l[1].wait_recv()
    over_cross[1].wait_recv()
    to_twin_core(1, 1 - h)
    climb(0)
    cross_l[2].wait_recv()
    over_cross[2].wait_recv()
    to_twin_core(2, 1 - h)
    spread_flat(every, 0, 1)
    climb(1)
    step_on(1)
    spread_flat(every, 0, 2)
    climb(2)

    mixed[0:5] = nn(w_zero[...].reshape(5 * local, 5 * C), flat_zero[:, 0:edges]).reshape(
        5, local, edges
    )
    for w, flat, start, blocks in ((w_one, flat_one, 5, 4), (w_two, flat_two, 13, 3)):
        size = blocks * C
        both = flat[:, 0 : 2 * edges]
        real = nn(w[0].reshape(blocks * local, size), both)
        imag = nn(w[1].reshape(blocks * local, size), both)
        mixed[start : start + blocks] = (real[:, :edges] - imag[:, edges:]).reshape(
            blocks, local, edges
        )
        mixed[start + blocks : start + 2 * blocks] = (
            real[:, edges:] + imag[:, :edges]
        ).reshape(blocks, local, edges)
    total = jnp.zeros((1, edges), F32)
    for j in range(19):
        total = total + jnp.sum(mixed[j] * grads[j].astype(F32), axis=0, keepdims=True)
    tally[...] = jnp.broadcast_to(total, tally.shape)
    counted = [net.copy(tally, tallies.at[i], d) for i, d in enumerate(chan_peers)]

    climb_on(0)
    scale = weight[...] * inverse
    for j in range(19):
        mixed[j] = mixed[j] * scale
    for l in range(5):
        for k in range(l * l, (l + 1) * (l + 1)):
            message[k] = rotate_out(rot, mixed, k, l).astype(BF16)
    update[...] = (
        nt(message[...].reshape(count, edges), arrive).reshape(25, local, atoms).astype(BF16)
    )
    climb_on(1)
    climbed(0)
    climb_on(2)
    for one in steps[1][2:]:
        one.wait_recv()
    for j in range(19):
        mixed[j] = own_sum(1, j)

    for one in counted:
        one.wait_recv()
    tally_sum = tally[...]
    for i in range(7):
        tally_sum = tally_sum + tallies[i]
    for one in fars:
        one.wait_recv()
    for j in range(19):
        mixed[j] = mixed[j] + far[j].astype(F32)
    for l in range(5):
        for k in range(l * l, (l + 1) * (l + 1)):
            message[k] = rotate_out(rot, mixed, k, l).astype(BF16)
    flat = message[...].reshape(count, edges)
    leaving[...] = nt(near, flat).astype(BF16)

    def exact(left, right, dims):
        return lax.dot_general(
            left, right, (dims, ((), ())),
            precision=lax.Precision.HIGHEST, preferred_element_type=F32,
        )

    side = lax.broadcasted_iota(jnp.int32, (128, edges), 0)
    side = side + jnp.where(side < 16, atoms + 16, atoms - 16)
    side_hot = jnp.where(side == source[...], 1.0, 0.0)
    tally_out[...] = exact(tally_sum, side_hot, ((1,), (1,)))
    halo = [
        net.copy(leaving.at[16:32], returned.at[0:16], to_ahead),
        net.copy(leaving.at[0:16], returned.at[16:32], to_behind),
        net.copy(tally_out, tally_in.at[0], to_ahead),
        net.copy(tally_out, tally_in.at[1], to_behind),
    ]
    climbed(1)
    own[...] = nt(flat, here).reshape(25, local, atoms)
    tally_a = exact(tally_sum, here.astype(F32), ((1,), (1,)))
    climbed(2)
    for one in halo:
        one.wait_recv()
    settled[...] = tn(returned[...], face_hot).reshape(25, local, atoms)
    lane = lax.broadcasted_iota(jnp.int32, (8, 128), 1)
    tally_face = jnp.where(lane < 16, tally_in[0], tally_in[1])
    tally_a = tally_a + exact(tally_face[:, 0:32], face_hot.astype(F32), ((1,), (0,)))
    factor = inverse_a * inverse_a * inverse_a * tally_a[0:1, :] / (25 * C)
    for l in range(5):
        gain_l = gain_t[0:local, l : l + 1] * inverse_a
        for k in range(l * l, (l + 1) * (l + 1)):
            grad_embed[k] = (
                (own[k] + settled[k]) * gain_l - embed[k].astype(F32) * factor
            ).astype(BF16)
    for one in lines:
        one.wait_recv()
    for p, out, width in ((0, sum_one, 512), (1, sum_zero, 320), (2, sum_two, 384)):
        total = kept[p][...]
        for i in range(3):
            total = total + line[p][i].astype(F32)
        for tile in range(TILES[p]):
            begin, end = 128 * tile, min(128 * (tile + 1), width)
            out[:, begin:end] = total[tile * UNIT[p] : (tile + 1) * UNIT[p], 0 : end - begin]
    net.finish()


def shards(
    embed, gain, w_zero, w_one, w_two, rot_table, face_atoms, edge_source, edge_target,
    rot_index, edge_weight, cotangent,
):
    atoms = embed.shape[2]
    local = embed.shape[1]
    edges = edge_source.shape[0]
    row = lambda a: a.reshape(1, edges)
    vmem = pl.BlockSpec(memory_space=pltpu.VMEM)
    hbm = pl.BlockSpec(memory_space=pl.ANY)
    block = (19, local, edges)
    scratch = [
        (w_zero.shape, BF16),
        (w_one.shape, BF16),
        (w_two.shape, BF16),
        ((128, 128), F32),
        ((128, 128), F32),
        ((32, 25 * local), BF16),
        ((32, 25 * local), BF16),
        ((25, 19, edges), F32),
        ((25, local, edges), F32),
        (block, BF16),
        (block, BF16),
        ((8, edges), F32),
        ((7, 8, edges), F32),
        ((19, 4, 2, local, edges), BF16),
        ((19, 4, 2, local, edges), BF16),
        ((19, 4, 2, local, edges), BF16),
        ((2, 10, local, edges), BF16),
        ((2, 9, local, edges), BF16),
        ((2, 19, local, edges), BF16),
        ((2, 19, local, edges), BF16),
        (block, BF16),
        (block, BF16),
        (block, BF16),
        (block, BF16),
        ((5 * C, 2 * edges), BF16),
        ((4 * C, 4 * edges), BF16),
        ((3 * C, 4 * edges), BF16),
        ((1280, 2 * edges), BF16),
        ((1024, 4 * edges), BF16),
        ((768, 4 * edges), BF16),
        ((384, 2 * edges), BF16),
        ((512, 4 * edges), BF16),
        ((384, 4 * edges), BF16),
    ]
    for p in range(3):
        rows = UNIT[p] * TILES[p]
        scratch += [
            ((4, 4, rows, 128), BF16),
            ((4, SPLIT[p], 128), BF16),
            ((4, rows - SPLIT[p], 128), BF16),
            ((4, rows, 128), BF16),
            ((4, rows, 128), BF16),
            ((3, rows, 128), BF16),
            ((3, rows, 128), BF16),
            ((rows, 128), F32),
        ]
    scratch += [
        (block, F32),
        ((25, local, edges), BF16),
        ((8, edges), F32),
        ((7, 8, edges), F32),
        ((25, local, atoms), F32),
        ((32, 25 * local), BF16),
        ((32, 25 * local), BF16),
        ((8, 128), F32),
        ((2, 8, 128), F32),
        ((25, local, atoms), F32),
    ]
    update, grad_embed, sum_zero, sum_one, sum_two = pl.pallas_call(
        layer_kernel,
        name="layer",
        out_shape=[
            jax.ShapeDtypeStruct((25, local, atoms), BF16),
            jax.ShapeDtypeStruct((25, local, atoms), BF16),
            jax.ShapeDtypeStruct((80, 5 * local), F32),
            jax.ShapeDtypeStruct((64, 8 * local), F32),
            jax.ShapeDtypeStruct((48, 6 * local), F32),
        ],
        in_specs=[vmem] * 9 + [hbm] * 3,
        out_specs=[vmem] * 5,
        scratch_shapes=[pltpu.VMEM(s, t) for s, t in scratch]
        + [
            pltpu.SemaphoreType.DMA((COPIES,)),
            pltpu.SemaphoreType.DMA((COPIES,)),
            pltpu.SemaphoreType.DMA((3,)),
        ],
        compiler_params=pltpu.CompilerParams(
            vmem_limit_bytes=VMEM_LIMIT, collective_id=0, has_side_effects=True
        ),
    )(
        embed, cotangent, gain, rot_table.transpose(1, 0, 2), face_atoms.reshape(1, -1),
        row(edge_source), row(edge_target), row(rot_index), row(edge_weight),
        w_zero, w_one, w_two,
    )

    grad_zero = sum_zero.T.reshape(5, local, 80)
    grad_one = sum_one.T.reshape(2, 4, local, 64)
    grad_two = sum_two.T.reshape(2, 3, local, 48)
    return (update, grad_embed, grad_zero, grad_one, grad_two)


def solution(mesh):
    torus = Mesh(mesh.devices.reshape(4, 4, 2, 4, 2), ("y", "z", "core", "x", "zh"))
    return jax.shard_map(
        shards,
        mesh=torus,
        in_specs=(
            P(None, CHAN, GRAPH),
            P(None, CHAN),
            P(None, CHAN, None),
            P(None, None, CHAN, None),
            P(None, None, CHAN, None),
            P(),
            P(GRAPH),
            P(GRAPH),
            P(GRAPH),
            P(GRAPH),
            P(GRAPH),
            P(None, CHAN, GRAPH),
        ),
        out_specs=(
            P(None, CHAN, GRAPH),
            P(None, CHAN, GRAPH),
            P(None, CHAN, GRAPH),
            P(None, None, CHAN, GRAPH),
            P(None, None, CHAN, GRAPH),
        ),
        check_vma=False,
    )
```

time: 105 us -> 96.5 us (0.919)
  the two profiles are of different devices: /device:TPU:64 before, /device:TPU:1 now
where the time goes in v2:
time: 96.5 us; the launch traced here: 95.8 us
  Pallas kernels  87.4 us (91%)
  local copies, waits for them, and re-layouts  7.71 us (8%)
    pallas_call x1, Pallas kernels, shards(): pl.pallas_call(layer_kernel, name='layer', out_shape=[jax.ShapeDtypeStruc...  87.4 us
    unnamed x6, local copies, waits for them, and re-layouts  4.96 us

profile of v2, /device:TPU:1, one launch (start us, length us, event | category | flops | bytes accessed | tf_op | source)
XLA Modules:
  0.0 95.8 jit_solution(13078088892181441970)
XLA Ops:
  0.6 87.4 %layer.1 = (bf16[25,64,128]{2,1,0:T(8,128)(2,1)}, bf16[25,64,128]{2,1,0:T(8,128)(2,1)}, f32[80,320]{1,0:T(8,128)}, f32[64,512]{1,0:T(8,128)}, f32[48,384]{1,0:T(8,128)}) custom-call(bf16[25,64,128]{2,1,0:T(8,128)(2,1)} %embed.1, bf16[25,64,128]{2,1,0:T(8,128)(2,1)} %cotangent.1, f32[5,64]{1,0:T(8,128)} %gain.1, f32[25,19,256]{2,1,0:T(8,128)} %bitcast.13, ...), custom_call_target="tpu_custom_call" | custom-call | tf_op jit(solution)/shard_map/layer/pallas_call | solution.py:608
  88.0 0.0 copy-start
  88.1 1.1 %reshape.41 = f32[2,3,64,48]{2,1,0,3:T(4,128)S(1)} reshape(f32[384,48]{0,1:T(8,128)} %bitcast.18) | data formatting | bytes 147456 | tf_op jit(solution)/shard_map/reshape | solution.py:637
  89.1 0.7 copy.22
  89.8 1.7 %copy.23 = f32[512,64]{1,0:T(8,128)} copy(f32[512,64]{0,1:T(8,128)} %bitcast.16) | data formatting | bytes 262144
  91.6 1.7 %copy.20 = f32[320,80]{1,0:T(8,128)} copy(f32[320,80]{0,1:T(8,128)} %bitcast.17) | data formatting | bytes 204800 | tf_op jit(solution)/shard_map/transpose | solution.py:635
  93.2 1.8 %copy.26 = bf16[25,64,128]{2,1,0:T(8,128)(2,1)} copy(bf16[25,64,128]{2,1,0:T(8,128)(2,1)} %get-tuple-element.30) | data formatting | bytes 819200
  95.0 0.0 copy-done
  95.0 0.8 copy.27
Async XLA Ops:
  88.0 7.0 %copy-start = (bf16[25,64,128]{2,1,0:T(8,128)(2,1)S(1)}, bf16[25,64,128]{2,1,0:T(8,128)(2,1)}, u32[]{:S(2)}) copy-start(bf16[25,64,128]{2,1,0:T(8,128)(2,1)} %get-tuple-element.31) | copy-start | bytes 1228804

commit v3 on v2

--- a/solution.py
+++ b/solution.py
@@ -14,7 +14,8 @@
 ROWS = tuple(tuple(j for j in range(19) if DEGREE[j] == l) for l in range(5))
 F32 = jnp.float32
 BF16 = jnp.bfloat16
-VMEM_LIMIT = 60 * 1024 * 1024
+VMEM_LIMIT = 46 * 1024 * 1024
+FINISH_LIMIT = 8 * 1024 * 1024
 MESH = pl.DeviceIdType.MESH
 PIECES = (slice(5, 13), slice(0, 5), slice(13, 19))
 HALF = (slice(0, 10), slice(10, 19))
@@ -86,9 +87,10 @@
 
 
 def layer_kernel(
-    embed, cotangent, gain, rot_table, face,
-    source, target, spin, weight, w_zero_hbm, w_one_hbm, w_two_hbm,
+    embed_hbm, cotangent_hbm, gain_hbm, rot_table_hbm, face_hbm,
+    source_hbm, target_hbm, spin_hbm, weight_hbm, w_zero_hbm, w_one_hbm, w_two_hbm,
     update, grad_embed, sum_zero, sum_one, sum_two,
+    embed, cotangent, gain, rot_table, face, source, target, spin, weight,
     w_zero, w_one, w_two, corner, gain_t, faces, halo_t, rot, values, grads, mine, square, squares, every, twin,
     back, relay_left, relay_right, from_left, from_right, to_far, far,
     scaled, scaled_twin, flat_zero, flat_one, flat_two, sel_zero, sel_one, sel_two,
@@ -135,7 +137,20 @@
     loads = [
         pltpu.make_async_copy(a, b, load.at[i])
         for i, (a, b) in enumerate(
-            ((w_zero_hbm, w_zero), (w_one_hbm, w_one), (w_two_hbm, w_two))
+            (
+                (embed_hbm, embed),
+                (face_hbm, face),
+                (rot_table_hbm, rot_table),
+                (gain_hbm, gain),
+                (source_hbm, source),
+                (target_hbm, target),
+                (spin_hbm, spin),
+                (weight_hbm, weight),
+                (cotangent_hbm, cotangent),
+                (w_zero_hbm, w_zero),
+                (w_one_hbm, w_one),
+                (w_two_hbm, w_two),
+            )
         )
     ]
     for one in loads:
@@ -146,6 +161,8 @@
     for device in partners:
         pl.semaphore_signal(barrier, inc=1, device_id=device, device_id_type=MESH)
 
+    for one in loads[:2]:
+        one.wait()
     corner[...] = jnp.zeros_like(corner)
     corner[0:1, 0:32] = face[...].astype(F32)
     face_col = jnp.broadcast_to(corner[0:1, :], (128, 128)).T[0:32].astype(jnp.int32)
@@ -159,6 +176,8 @@
         net.copy(faces.at[0:16], halo_t.at[16:32], to_behind),
     ]
 
+    for one in loads[2:8]:
+        one.wait()
     corner[0:5, 0:local] = gain[...]
     gain_t[...] = corner[...].T
     turn = hot(spin[...], rot_table.shape[2])
@@ -172,21 +191,26 @@
         one = embed[k].astype(F32)
         total_a = total_a + jnp.sum(one * one, axis=0, keepdims=True)
     here = hot(source[...], atoms)
-    near = hot(source[...], 32, atoms)
+    near_hot = hot(source[...], 32, atoms)
 
     for one in halo:
         one.wait_recv()
-    values[...] = (nn(flat_embed, here) + tn(halo_t[...], near)).reshape(25, local, edges)
+    values[...] = (nn(flat_embed, here) + tn(halo_t[...], near_hot)).reshape(25, local, edges)
     for j in range(19):
         l = DEGREE[j]
         mine[j] = (rotate_in(rot, values, j) * gain_t[0:local, l : l + 1]).astype(BF16)
     cross, near_r, near_l = [], [], []
-    for p in range(3):
+
+    def near(p):
         here_at = mine.at[PIECES[p]]
         there_at = every.at[PIECES[p], x, h]
-        cross.append(net.copy(here_at, there_at, to_far_half))
         near_r.append(net.copy(here_at, there_at, to_xr))
         near_l.append(net.copy(here_at, there_at, to_xl))
+
+    for p in range(3):
+        cross.append(net.copy(mine.at[PIECES[p]], every.at[PIECES[p], x, h], to_far_half))
+        if p == 0:
+            near(0)
     total_e = jnp.zeros((1, edges), F32)
     for k in range(25):
         one = values[k]
@@ -196,12 +220,13 @@
     for j in range(19):
         every[j, x, h] = mine[j]
 
+    loads[8].wait()
     arrive = hot(target[...], atoms)
     values[...] = nn(cotangent[...].reshape(count, atoms), arrive).reshape(25, local, edges)
     for j in range(19):
         grads[j] = (rotate_in(rot, values, j) * weight[...]).astype(BF16)
 
-    for one in loads:
+    for one in loads[9:]:
         one.wait()
     back[0:5] = tn(
         w_zero[...].reshape(5 * local, 5 * C), grads[0:5].reshape(5 * local, edges)
@@ -237,7 +262,7 @@
             net.copy(back.at[HALF[0], xl, to], from_right.at[q, HALF[0]], to_xl),
         ]
 
-    def step_on(q):
+    def step_right(q):
         to = half[q]
         steps[q][0].wait_recv()
         for j in range(10):
@@ -245,6 +270,9 @@
         steps[q].append(
             net.copy(back.at[HALF[0], xr, to], from_left.at[q, HALF[0]], to_xr)
         )
+
+    def step_left(q):
+        to = half[q]
         steps[q][1].wait_recv()
         for j in range(10, 19):
             back[j, xl, to] = added(back[j, xl, to], relay_right[q, j - 10])
@@ -278,68 +306,6 @@
     def to_twin_core(p, h_from):
         block = every.at[PIECES[p], :, h_from]
         twins[p].append(net.copy(block, twin.at[PIECES[p], :, h_from], to_twin))
-
-    step(0)
-    near_r[0].wait_recv()
-    over_own[0] = forward(0, xl, h, to_xr)
-    near_l[1].wait_recv()
-    over_own[1] = forward(1, xr, h, to_xl)
-    near_l[2].wait_recv()
-    over_own[2] = forward(2, xr, h, to_xl)
-    cross[0].wait_recv()
-    cross_r[0] = forward(0, x, 1 - h, to_xr)
-    cross_l[0] = forward(0, x, 1 - h, to_xl)
-    step_on(0)
-    cross[1].wait_recv()
-    cross_r[1] = forward(1, x, 1 - h, to_xr)
-    cross_l[1] = forward(1, x, 1 - h, to_xl)
-
-    for one in asked:
-        one.wait_recv()
-    square_sum = square[...]
-    for i in range(7):
-        square_sum = square_sum + squares[i]
-    inverse_both = lax.rsqrt(square_sum / (25 * C) + EPSILON)
-    inverse, inverse_a = inverse_both[0:1, :], inverse_both[1:2, :]
-    for j in range(19):
-        scaled[j] = (grads[j].astype(F32) * inverse).astype(BF16)
-    scaled_copy = net.copy(scaled, scaled_twin, to_twin)
-
-    def right_side(buffer, lane):
-        wide = 5 * local
-        right_zero[0:wide, lane * edges : (lane + 1) * edges] = buffer[0:5].reshape(wide, edges)
-        for right, start, blocks in ((right_one, 5, 4), (right_two, 13, 3)):
-            rows = blocks * local
-            plus = buffer[start : start + blocks].reshape(rows, edges)
-            minus = buffer[start + blocks : start + 2 * blocks].reshape(rows, edges)
-            at = 2 * lane * edges
-            right[0:rows, at : at + edges] = plus
-            right[0:rows, at + edges : at + 2 * edges] = minus
-            right[rows : 2 * rows, at : at + edges] = minus
-            right[rows : 2 * rows, at + edges : at + 2 * edges] = -plus
-
-    right_zero[...] = jnp.zeros_like(right_zero)
-    right_side(scaled, 0)
-
-    cross[2].wait_recv()
-    cross_r[2] = forward(2, x, 1 - h, to_xr)
-    cross_l[2] = forward(2, x, 1 - h, to_xl)
-    near_l[0].wait_recv()
-    over_own[0].wait_recv()
-    to_twin_core(0, h)
-    for p in (1, 2):
-        near_r[p].wait_recv()
-        over_own[p].wait_recv()
-        to_twin_core(p, h)
-    cross_l[0].wait_recv()
-    over_cross[0] = forward(0, xr, 1 - h, to_xl)
-    send_far(0)
-    cross_r[1].wait_recv()
-    over_cross[1] = forward(1, xl, 1 - h, to_xr)
-    send_far(1)
-    cross_r[2].wait_recv()
-    over_cross[2] = forward(2, xl, 1 - h, to_xr)
-    step(1)
 
     flats = (flat_one, flat_zero, flat_two)
     sels = (sel_one, sel_zero, sel_two)
@@ -418,24 +384,85 @@
             else:
                 kept[p][...] = total
 
+    def right_side(buffer, lane):
+        wide = 5 * local
+        right_zero[0:wide, lane * edges : (lane + 1) * edges] = buffer[0:5].reshape(wide, edges)
+        for right, start, blocks in ((right_one, 5, 4), (right_two, 13, 3)):
+            rows = blocks * local
+            plus = buffer[start : start + blocks].reshape(rows, edges)
+            minus = buffer[start + blocks : start + 2 * blocks].reshape(rows, edges)
+            at = 2 * lane * edges
+            right[0:rows, at : at + edges] = plus
+            right[0:rows, at + edges : at + 2 * edges] = minus
+            right[rows : 2 * rows, at : at + edges] = minus
+            right[rows : 2 * rows, at + edges : at + 2 * edges] = -plus
+
+    step(0)
+    near_r[0].wait_recv()
+    over_own[0] = forward(0, xl, h, to_xr)
+    cross[0].wait_recv()
+    cross_r[0] = forward(0, x, 1 - h, to_xr)
+    cross_l[0] = forward(0, x, 1 - h, to_xl)
+    step_right(0)
+    cross_l[0].wait_recv()
+    over_cross[0] = forward(0, xr, 1 - h, to_xl)
+    step_left(0)
+    near(1)
+    near(2)
+    near_l[0].wait_recv()
+    over_own[0].wait_recv()
+    to_twin_core(0, h)
+    for p in (1, 2):
+        cross[p].wait_recv()
+        cross_r[p] = forward(p, x, 1 - h, to_xr)
+        cross_l[p] = forward(p, x, 1 - h, to_xl)
+    for one in asked:
+        one.wait_recv()
+    square_sum = square[...]
+    for i in range(7):
+        square_sum = square_sum + squares[i]
+    inverse_both = lax.rsqrt(square_sum / (25 * C) + EPSILON)
+    inverse, inverse_a = inverse_both[0:1, :], inverse_both[1:2, :]
+    for j in range(19):
+        scaled[j] = (grads[j].astype(F32) * inverse).astype(BF16)
+    scaled_copy = net.copy(scaled, scaled_twin, to_twin)
+
+    right_zero[...] = jnp.zeros_like(right_zero)
+    right_side(scaled, 0)
+
+    scaled_copy.wait_recv()
+    right_side(scaled_twin, 1)
     cross_r[0].wait_recv()
     over_cross[0].wait_recv()
     to_twin_core(0, 1 - h)
     spread_flat(every, 0, 0)
-    scaled_copy.wait_recv()
-    right_side(scaled_twin, 1)
+    send_far(0)
+    climb(0)
+    send_far(1)
+    for p in (1, 2):
+        near_l[p].wait_recv()
+        over_own[p] = forward(p, xr, h, to_xl)
+    for p in (1, 2):
+        cross_r[p].wait_recv()
+        over_cross[p] = forward(p, xl, 1 - h, to_xr)
+    step(1)
+    climb_on(0)
+    near_r[1].wait_recv()
+    over_own[1].wait_recv()
+    to_twin_core(1, h)
     cross_l[1].wait_recv()
     over_cross[1].wait_recv()
     to_twin_core(1, 1 - h)
-    climb(0)
+    spread_flat(every, 0, 1)
+    climb(1)
+    near_r[2].wait_recv()
+    over_own[2].wait_recv()
+    to_twin_core(2, h)
     cross_l[2].wait_recv()
     over_cross[2].wait_recv()
     to_twin_core(2, 1 - h)
-    spread_flat(every, 0, 1)
-    climb(1)
-    step_on(1)
     spread_flat(every, 0, 2)
-    climb(2)
+    climbed(0)
 
     mixed[0:5] = nn(w_zero[...].reshape(5 * local, 5 * C), flat_zero[:, 0:edges]).reshape(
         5, local, edges
@@ -457,7 +484,11 @@
     tally[...] = jnp.broadcast_to(total, tally.shape)
     counted = [net.copy(tally, tallies.at[i], d) for i, d in enumerate(chan_peers)]
 
-    climb_on(0)
+    step_right(1)
+    step_left(1)
+    climb_on(1)
+    climb(2)
+
     scale = weight[...] * inverse
     for j in range(19):
         mixed[j] = mixed[j] * scale
@@ -467,8 +498,7 @@
     update[...] = (
         nt(message[...].reshape(count, edges), arrive).reshape(25, local, atoms).astype(BF16)
     )
-    climb_on(1)
-    climbed(0)
+    climbed(1)
     climb_on(2)
     for one in steps[1][2:]:
         one.wait_recv()
@@ -488,7 +518,7 @@
         for k in range(l * l, (l + 1) * (l + 1)):
             message[k] = rotate_out(rot, mixed, k, l).astype(BF16)
     flat = message[...].reshape(count, edges)
-    leaving[...] = nt(near, flat).astype(BF16)
+    leaving[...] = nt(near_hot, flat).astype(BF16)
 
     def exact(left, right, dims):
         return lax.dot_general(
@@ -506,7 +536,6 @@
         net.copy(tally_out, tally_in.at[0], to_ahead),
         net.copy(tally_out, tally_in.at[1], to_behind),
     ]
-    climbed(1)
     own[...] = nt(flat, here).reshape(25, local, atoms)
     tally_a = exact(tally_sum, here.astype(F32), ((1,), (1,)))
     climbed(2)
@@ -525,7 +554,7 @@
             ).astype(BF16)
     for one in lines:
         one.wait_recv()
-    for p, out, width in ((0, sum_one, 512), (1, sum_zero, 320), (2, sum_two, 384)):
+    for p, out, width in ((0, sum_one, 512), (1, sum_zero, 384), (2, sum_two, 384)):
         total = kept[p][...]
         for i in range(3):
             total = total + line[p][i].astype(F32)
@@ -533,6 +562,25 @@
             begin, end = 128 * tile, min(128 * (tile + 1), width)
             out[:, begin:end] = total[tile * UNIT[p] : (tile + 1) * UNIT[p], 0 : end - begin]
     net.finish()
+
+
+def finish_kernel(
+    update_in, grad_in, sum_zero, sum_one, sum_two, update, grad, grad_zero, grad_one, grad_two
+):
+    update[...] = update_in[...]
+    grad[...] = grad_in[...]
+    local = grad_zero.shape[1]
+    for t in range(2):
+        turned = sum_zero[:, 128 * t : 128 * (t + 1)].T
+        grad_zero[2 * t] = turned[:local]
+        grad_zero[2 * t + 1] = turned[local:]
+    grad_zero[4] = sum_zero[:, 256:384].T[:local]
+    for t in range(4):
+        turned = sum_one[:, 128 * t : 128 * (t + 1)].T
+        for i in (0, 1):
+            grad_one[(2 * t + i) // 4, (2 * t + i) % 4] = turned[i * local : (i + 1) * local]
+    for i in range(6):
+        grad_two[i // 3, i % 3] = sum_two[:, i * local : (i + 1) * local]
 
 
 def shards(
@@ -544,9 +592,15 @@
     edges = edge_source.shape[0]
     row = lambda a: a.reshape(1, edges)
     vmem = pl.BlockSpec(memory_space=pltpu.VMEM)
-    hbm = pl.BlockSpec(memory_space=pl.ANY)
+    hbm = pl.BlockSpec(memory_space=pltpu.HBM)
     block = (19, local, edges)
-    scratch = [
+    args = (
+        embed, cotangent, gain, rot_table.transpose(1, 0, 2), face_atoms.reshape(1, -1),
+        row(edge_source), row(edge_target), row(rot_index), row(edge_weight),
+        w_zero, w_one, w_two,
+    )
+    scratch = [(a.shape, a.dtype) for a in args[:9]]
+    scratch += [
         (w_zero.shape, BF16),
         (w_one.shape, BF16),
         (w_two.shape, BF16),
@@ -611,31 +665,37 @@
         out_shape=[
             jax.ShapeDtypeStruct((25, local, atoms), BF16),
             jax.ShapeDtypeStruct((25, local, atoms), BF16),
-            jax.ShapeDtypeStruct((80, 5 * local), F32),
+            jax.ShapeDtypeStruct((80, 384), F32),
             jax.ShapeDtypeStruct((64, 8 * local), F32),
             jax.ShapeDtypeStruct((48, 6 * local), F32),
         ],
-        in_specs=[vmem] * 9 + [hbm] * 3,
+        in_specs=[hbm] * 12,
         out_specs=[vmem] * 5,
         scratch_shapes=[pltpu.VMEM(s, t) for s, t in scratch]
         + [
             pltpu.SemaphoreType.DMA((COPIES,)),
             pltpu.SemaphoreType.DMA((COPIES,)),
-            pltpu.SemaphoreType.DMA((3,)),
+            pltpu.SemaphoreType.DMA((12,)),
         ],
         compiler_params=pltpu.CompilerParams(
             vmem_limit_bytes=VMEM_LIMIT, collective_id=0, has_side_effects=True
         ),
-    )(
-        embed, cotangent, gain, rot_table.transpose(1, 0, 2), face_atoms.reshape(1, -1),
-        row(edge_source), row(edge_target), row(rot_index), row(edge_weight),
-        w_zero, w_one, w_two,
-    )
-
-    grad_zero = sum_zero.T.reshape(5, local, 80)
-    grad_one = sum_one.T.reshape(2, 4, local, 64)
-    grad_two = sum_two.T.reshape(2, 3, local, 48)
-    return (update, grad_embed, grad_zero, grad_one, grad_two)
+    )(*(pltpu.with_memory_space_constraint(a, pltpu.HBM) for a in args))
+    *outs, grad_two = pl.pallas_call(
+        finish_kernel,
+        name="finish",
+        out_shape=[
+            jax.ShapeDtypeStruct((25, local, atoms), BF16),
+            jax.ShapeDtypeStruct((25, local, atoms), BF16),
+            jax.ShapeDtypeStruct((5, local, 80), F32),
+            jax.ShapeDtypeStruct((2, 4, local, 64), F32),
+            jax.ShapeDtypeStruct((2, 3, 48, local), F32),
+        ],
+        in_specs=[vmem] * 5,
+        out_specs=[vmem] * 5,
+        compiler_params=pltpu.CompilerParams(vmem_limit_bytes=FINISH_LIMIT),
+    )(update, grad_embed, sum_zero, sum_one, sum_two)
+    return (*outs, grad_two.transpose(0, 1, 3, 2))
 
 
 def solution(mesh):

time: 96.5 us -> 74.8 us (0.78)
  Pallas kernels: 87.4 us -> 73.2 us
  local copies, waits for them, and re-layouts: 7.71 us -> 0 us
    pallas_call x1, Pallas kernels: 87.4 us -> 71.9 us  [shards(): pl.pallas_call(layer_kernel, name='layer', out_shape=[jax.ShapeDtypeStruc...]
    unnamed x6 -> x0, local copies, waits for them, and re-layouts: 4.96 us -> none
    transpose x1 -> x0, local copies, waits for them, and re-layouts: 1.68 us -> none  [shards(): grad_zero = sum_zero.T.reshape(5, local, 80)]
    pallas_call x0 -> x1, Pallas kernels: none -> 1.23 us  [shards(): pl.pallas_call(finish_kernel, name='finish', out_shape=[jax.ShapeDtypeStr...]
    reshape x1 -> x0, local copies, waits for them, and re-layouts: 1.06 us -> none  [shards(): grad_two = sum_two.T.reshape(2, 3, local, 48)]
where the time goes in v3:
time: 74.8 us; the launch traced here: 73.8 us
  Pallas kernels  73.2 us (98%)
    pallas_call x1, Pallas kernels, shards(): pl.pallas_call(layer_kernel, name='layer', out_shape=[jax.ShapeDtypeStruc...  71.9 us

profile of v3, /device:TPU:1, one launch (start us, length us, event | category | flops | bytes accessed | tf_op | source)
XLA Modules:
  0.0 73.8 jit_solution(7570280449332490407)
XLA Ops:
  0.6 71.9 %layer.1 = (bf16[25,64,128]{2,1,0:T(8,128)(2,1)S(1)}, bf16[25,64,128]{2,1,0:T(8,128)(2,1)S(1)}, f32[80,384]{1,0:T(8,128)S(1)}, f32[64,512]{1,0:T(8,128)S(1)}, f32[48,384]{1,0:T(8,128)S(1)}) custom-call(bf16[25,64,128]{2,1,0:T(8,128)(2,1)} %embed_hbm.1, bf16[25,64,128]{2,1,0:T(8,128)(2,1)} %cotangent_hbm.1, f32[5,64]{1,0:T(8,128)} %gain_hbm.1, ...), custom_call_target="tpu_custom_call" | custom-call | tf_op jit(solution)/shard_map/layer/pallas_call | solution.py:662
  72.6 1.2 %finish.1 = (bf16[25,64,128]{2,1,0:T(8,128)(2,1)}, bf16[25,64,128]{2,1,0:T(8,128)(2,1)}, f32[5,64,80]{2,1,0:T(8,128)}, f32[2,4,64,64]{3,2,1,0:T(8,128)}, f32[2,3,48,64]{3,2,1,0:T(8,128)}) custom-call(bf16[25,64,128]{2,1,0:T(8,128)(2,1)S(1)} %get-tuple-element.15.update_in, bf16[25,64,128]{2,1,0:T(8,128)(2,1)S(1)} %get-tuple-element.16.grad_in, ...), custom_call_target="tpu_custom_call" | custom-call | tf_op jit(solution)/shard_map/finish/pallas_call | solution.py:684

commit v4 on v3

--- a/solution.py
+++ b/solution.py
@@ -193,33 +193,6 @@
     here = hot(source[...], atoms)
     near_hot = hot(source[...], 32, atoms)
 
-    for one in halo:
-        one.wait_recv()
-    values[...] = (nn(flat_embed, here) + tn(halo_t[...], near_hot)).reshape(25, local, edges)
-    for j in range(19):
-        l = DEGREE[j]
-        mine[j] = (rotate_in(rot, values, j) * gain_t[0:local, l : l + 1]).astype(BF16)
-    cross, near_r, near_l = [], [], []
-
-    def near(p):
-        here_at = mine.at[PIECES[p]]
-        there_at = every.at[PIECES[p], x, h]
-        near_r.append(net.copy(here_at, there_at, to_xr))
-        near_l.append(net.copy(here_at, there_at, to_xl))
-
-    for p in range(3):
-        cross.append(net.copy(mine.at[PIECES[p]], every.at[PIECES[p], x, h], to_far_half))
-        if p == 0:
-            near(0)
-    total_e = jnp.zeros((1, edges), F32)
-    for k in range(25):
-        one = values[k]
-        total_e = total_e + jnp.sum(one * one, axis=0, keepdims=True)
-    square[...] = jnp.concatenate([total_e, total_a, jnp.zeros((6, edges), F32)], axis=0)
-    asked = [net.copy(square, squares.at[i], d) for i, d in enumerate(chan_peers)]
-    for j in range(19):
-        every[j, x, h] = mine[j]
-
     loads[8].wait()
     arrive = hot(target[...], atoms)
     values[...] = nn(cotangent[...].reshape(count, atoms), arrive).reshape(25, local, edges)
@@ -253,14 +226,48 @@
     half = (1 - h, h)
     steps = [[], []]
 
-    def step(q):
+    def step_over(q):
         to = half[q]
         steps[q] = [
             net.copy(back.at[HALF[0], xo, to], relay_left.at[q], to_xr),
             net.copy(back.at[HALF[1], xo, to], relay_right.at[q], to_xl),
+        ]
+
+    def step_next(q):
+        to = half[q]
+        steps[q] += [
             net.copy(back.at[HALF[1], xr, to], from_left.at[q, HALF[1]], to_xr),
             net.copy(back.at[HALF[0], xl, to], from_right.at[q, HALF[0]], to_xl),
         ]
+
+    step_over(0)
+    for one in halo:
+        one.wait_recv()
+    values[...] = (nn(flat_embed, here) + tn(halo_t[...], near_hot)).reshape(25, local, edges)
+    for j in range(19):
+        l = DEGREE[j]
+        mine[j] = (rotate_in(rot, values, j) * gain_t[0:local, l : l + 1]).astype(BF16)
+    cross, near_r, near_l = [], [], []
+
+    def near(p):
+        here_at = mine.at[PIECES[p]]
+        there_at = every.at[PIECES[p], x, h]
+        near_r.append(net.copy(here_at, there_at, to_xr))
+        near_l.append(net.copy(here_at, there_at, to_xl))
+
+    for p in range(3):
+        cross.append(net.copy(mine.at[PIECES[p]], every.at[PIECES[p], x, h], to_far_half))
+        if p == 0:
+            near(0)
+    step_next(0)
+    total_e = jnp.zeros((1, edges), F32)
+    for k in range(25):
+        one = values[k]
+        total_e = total_e + jnp.sum(one * one, axis=0, keepdims=True)
+    square[...] = jnp.concatenate([total_e, total_a, jnp.zeros((6, edges), F32)], axis=0)
+    asked = [net.copy(square, squares.at[i], d) for i, d in enumerate(chan_peers)]
+    for j in range(19):
+        every[j, x, h] = mine[j]
 
     def step_right(q):
         to = half[q]
@@ -397,25 +404,25 @@
             right[rows : 2 * rows, at : at + edges] = minus
             right[rows : 2 * rows, at + edges : at + 2 * edges] = -plus
 
-    step(0)
     near_r[0].wait_recv()
     over_own[0] = forward(0, xl, h, to_xr)
     cross[0].wait_recv()
     cross_r[0] = forward(0, x, 1 - h, to_xr)
     cross_l[0] = forward(0, x, 1 - h, to_xl)
     step_right(0)
+    near(1)
     cross_l[0].wait_recv()
     over_cross[0] = forward(0, xr, 1 - h, to_xl)
     step_left(0)
-    near(1)
+    cross[1].wait_recv()
+    cross_r[1] = forward(1, x, 1 - h, to_xr)
+    cross_l[1] = forward(1, x, 1 - h, to_xl)
+    near_l[1].wait_recv()
+    over_own[1] = forward(1, xr, h, to_xl)
     near(2)
     near_l[0].wait_recv()
     over_own[0].wait_recv()
     to_twin_core(0, h)
-    for p in (1, 2):
-        cross[p].wait_recv()
-        cross_r[p] = forward(p, x, 1 - h, to_xr)
-        cross_l[p] = forward(p, x, 1 - h, to_xl)
     for one in asked:
         one.wait_recv()
     square_sum = square[...]
@@ -439,14 +446,11 @@
     send_far(0)
     climb(0)
     send_far(1)
-    for p in (1, 2):
-        near_l[p].wait_recv()
-        over_own[p] = forward(p, xr, h, to_xl)
-    for p in (1, 2):
-        cross_r[p].wait_recv()
-        over_cross[p] = forward(p, xl, 1 - h, to_xr)
-    step(1)
-    climb_on(0)
+    cross_r[1].wait_recv()
+    over_cross[1] = forward(1, xl, 1 - h, to_xr)
+    cross[2].wait_recv()
+    cross_r[2] = forward(2, x, 1 - h, to_xr)
+    cross_l[2] = forward(2, x, 1 - h, to_xl)
     near_r[1].wait_recv()
     over_own[1].wait_recv()
     to_twin_core(1, h)
@@ -454,7 +458,14 @@
     over_cross[1].wait_recv()
     to_twin_core(1, 1 - h)
     spread_flat(every, 0, 1)
+    climb_on(0)
+    near_l[2].wait_recv()
+    over_own[2] = forward(2, xr, h, to_xl)
     climb(1)
+    cross_r[2].wait_recv()
+    over_cross[2] = forward(2, xl, 1 - h, to_xr)
+    step_over(1)
+    step_next(1)
     near_r[2].wait_recv()
     over_own[2].wait_recv()
     to_twin_core(2, h)
@@ -463,6 +474,7 @@
     to_twin_core(2, 1 - h)
     spread_flat(every, 0, 2)
     climbed(0)
+    climb(2)
 
     mixed[0:5] = nn(w_zero[...].reshape(5 * local, 5 * C), flat_zero[:, 0:edges]).reshape(
         5, local, edges
@@ -487,7 +499,6 @@
     step_right(1)
     step_left(1)
     climb_on(1)
-    climb(2)
 
     scale = weight[...] * inverse
     for j in range(19):

time: 74.8 us -> 75.2 us (level); the launches traced: 73.8 us -> 75.2 us
  Pallas kernels: 73.2 us -> 74.5 us
    pallas_call x1, Pallas kernels: 71.9 us -> 73.3 us  [shards(): pl.pallas_call(layer_kernel, name='layer', out_shape=[jax.ShapeDtypeStruc...]
where the time goes in v4:
time: 75.2 us
  Pallas kernels  74.5 us (99%)
    pallas_call x1, Pallas kernels, shards(): pl.pallas_call(layer_kernel, name='layer', out_shape=[jax.ShapeDtypeStruc...  73.3 us

profile of v4, /device:TPU:1, one launch (start us, length us, event | category | flops | bytes accessed | tf_op | source)
XLA Modules:
  0.0 75.2 jit_solution(1172515341088352457)
XLA Ops:
  0.6 73.3 %layer.1 = (bf16[25,64,128]{2,1,0:T(8,128)(2,1)S(1)}, bf16[25,64,128]{2,1,0:T(8,128)(2,1)S(1)}, f32[80,384]{1,0:T(8,128)S(1)}, f32[64,512]{1,0:T(8,128)S(1)}, f32[48,384]{1,0:T(8,128)S(1)}) custom-call(bf16[25,64,128]{2,1,0:T(8,128)(2,1)} %embed_hbm.1, bf16[25,64,128]{2,1,0:T(8,128)(2,1)} %cotangent_hbm.1, f32[5,64]{1,0:T(8,128)} %gain_hbm.1, ...), custom_call_target="tpu_custom_call" | custom-call | tf_op jit(solution)/shard_map/layer/pallas_call | solution.py:673
  73.9 1.2 %finish.1 = (bf16[25,64,128]{2,1,0:T(8,128)(2,1)}, bf16[25,64,128]{2,1,0:T(8,128)(2,1)}, f32[5,64,80]{2,1,0:T(8,128)}, f32[2,4,64,64]{3,2,1,0:T(8,128)}, f32[2,3,48,64]{3,2,1,0:T(8,128)}) custom-call(bf16[25,64,128]{2,1,0:T(8,128)(2,1)S(1)} %get-tuple-element.15.update_in, bf16[25,64,128]{2,1,0:T(8,128)(2,1)S(1)} %get-tuple-element.16.grad_in, ...), custom_call_target="tpu_custom_call" | custom-call | tf_op jit(solution)/shard_map/finish/pallas_call | solution.py:695

commit v5 on v4

--- a/solution.py
+++ b/solution.py
@@ -193,6 +193,42 @@
     here = hot(source[...], atoms)
     near_hot = hot(source[...], 32, atoms)
 
+    values[...] = nn(flat_embed, here).reshape(25, local, edges)
+    for one in halo:
+        one.wait_recv()
+    values[...] += tn(halo_t[...], near_hot).reshape(25, local, edges)
+    cross, near_r, near_l = [], [], []
+
+    def near(p):
+        here_at = mine.at[PIECES[p]]
+        there_at = every.at[PIECES[p], x, h]
+        near_r.append(net.copy(here_at, there_at, to_xr))
+        near_l.append(net.copy(here_at, there_at, to_xl))
+
+    def over(p):
+        cross.append(net.copy(mine.at[PIECES[p]], every.at[PIECES[p], x, h], to_far_half))
+
+    def own_frames(p):
+        for j in range(19)[PIECES[p]]:
+            l = DEGREE[j]
+            one = (rotate_in(rot, values, j) * gain_t[0:local, l : l + 1]).astype(BF16)
+            mine[j] = one
+            every[j, x, h] = one
+
+    own_frames(0)
+    over(0)
+    near(0)
+    own_frames(1)
+    own_frames(2)
+    total_e = jnp.zeros((1, edges), F32)
+    for k in range(25):
+        one = values[k]
+        total_e = total_e + jnp.sum(one * one, axis=0, keepdims=True)
+    square[...] = jnp.concatenate([total_e, total_a, jnp.zeros((6, edges), F32)], axis=0)
+    asked = [net.copy(square, squares.at[i], d) for i, d in enumerate(chan_peers)]
+    over(1)
+    over(2)
+
     loads[8].wait()
     arrive = hot(target[...], atoms)
     values[...] = nn(cotangent[...].reshape(count, atoms), arrive).reshape(25, local, edges)
@@ -241,33 +277,7 @@
         ]
 
     step_over(0)
-    for one in halo:
-        one.wait_recv()
-    values[...] = (nn(flat_embed, here) + tn(halo_t[...], near_hot)).reshape(25, local, edges)
-    for j in range(19):
-        l = DEGREE[j]
-        mine[j] = (rotate_in(rot, values, j) * gain_t[0:local, l : l + 1]).astype(BF16)
-    cross, near_r, near_l = [], [], []
-
-    def near(p):
-        here_at = mine.at[PIECES[p]]
-        there_at = every.at[PIECES[p], x, h]
-        near_r.append(net.copy(here_at, there_at, to_xr))
-        near_l.append(net.copy(here_at, there_at, to_xl))
-
-    for p in range(3):
-        cross.append(net.copy(mine.at[PIECES[p]], every.at[PIECES[p], x, h], to_far_half))
-        if p == 0:
-            near(0)
     step_next(0)
-    total_e = jnp.zeros((1, edges), F32)
-    for k in range(25):
-        one = values[k]
-        total_e = total_e + jnp.sum(one * one, axis=0, keepdims=True)
-    square[...] = jnp.concatenate([total_e, total_a, jnp.zeros((6, edges), F32)], axis=0)
-    asked = [net.copy(square, squares.at[i], d) for i, d in enumerate(chan_peers)]
-    for j in range(19):
-        every[j, x, h] = mine[j]
 
     def step_right(q):
         to = half[q]
@@ -437,13 +447,13 @@
     right_zero[...] = jnp.zeros_like(right_zero)
     right_side(scaled, 0)
 
-    scaled_copy.wait_recv()
-    right_side(scaled_twin, 1)
     cross_r[0].wait_recv()
     over_cross[0].wait_recv()
     to_twin_core(0, 1 - h)
     spread_flat(every, 0, 0)
     send_far(0)
+    scaled_copy.wait_recv()
+    right_side(scaled_twin, 1)
     climb(0)
     send_far(1)
     cross_r[1].wait_recv()
@@ -473,8 +483,10 @@
     over_cross[2].wait_recv()
     to_twin_core(2, 1 - h)
     spread_flat(every, 0, 2)
+    climb_on(1)
+    step_right(1)
+    step_left(1)
     climbed(0)
-    climb(2)
 
     mixed[0:5] = nn(w_zero[...].reshape(5 * local, 5 * C), flat_zero[:, 0:edges]).reshape(
         5, local, edges
@@ -496,9 +508,7 @@
     tally[...] = jnp.broadcast_to(total, tally.shape)
     counted = [net.copy(tally, tallies.at[i], d) for i, d in enumerate(chan_peers)]
 
-    step_right(1)
-    step_left(1)
-    climb_on(1)
+    climb(2)
 
     scale = weight[...] * inverse
     for j in range(19):

time: 75.2 us -> 74.2 us (0.987)
  Pallas kernels: 74.5 us -> 73.5 us
    pallas_call x1, Pallas kernels: 73.3 us -> 72.3 us  [shards(): pl.pallas_call(layer_kernel, name='layer', out_shape=[jax.ShapeDtypeStruc...]
where the time goes in v5:
time: 74.2 us; the launch traced here: 74.1 us
  Pallas kernels  73.5 us (99%)
    pallas_call x1, Pallas kernels, shards(): pl.pallas_call(layer_kernel, name='layer', out_shape=[jax.ShapeDtypeStruc...  72.3 us

profile of v5, /device:TPU:1, one launch (start us, length us, event | category | flops | bytes accessed | tf_op | source)
XLA Modules:
  0.0 74.1 jit_solution(3806750411264116776)
XLA Ops:
  0.6 72.3 %layer.1 = (bf16[25,64,128]{2,1,0:T(8,128)(2,1)S(1)}, bf16[25,64,128]{2,1,0:T(8,128)(2,1)S(1)}, f32[80,384]{1,0:T(8,128)S(1)}, f32[64,512]{1,0:T(8,128)S(1)}, f32[48,384]{1,0:T(8,128)S(1)}) custom-call(bf16[25,64,128]{2,1,0:T(8,128)(2,1)} %embed_hbm.1, bf16[25,64,128]{2,1,0:T(8,128)(2,1)} %cotangent_hbm.1, f32[5,64]{1,0:T(8,128)} %gain_hbm.1, ...), custom_call_target="tpu_custom_call" | custom-call | tf_op jit(solution)/shard_map/layer/pallas_call | solution.py:683
  72.9 1.2 %finish.1 = (bf16[25,64,128]{2,1,0:T(8,128)(2,1)}, bf16[25,64,128]{2,1,0:T(8,128)(2,1)}, f32[5,64,80]{2,1,0:T(8,128)}, f32[2,4,64,64]{3,2,1,0:T(8,128)}, f32[2,3,48,64]{3,2,1,0:T(8,128)}) custom-call(bf16[25,64,128]{2,1,0:T(8,128)(2,1)S(1)} %get-tuple-element.15.update_in, bf16[25,64,128]{2,1,0:T(8,128)(2,1)S(1)} %get-tuple-element.16.grad_in, ...), custom_call_target="tpu_custom_call" | custom-call | tf_op jit(solution)/shard_map/finish/pallas_call | solution.py:705

commit v6 on v5

--- a/solution.py
+++ b/solution.py
@@ -483,10 +483,6 @@
     over_cross[2].wait_recv()
     to_twin_core(2, 1 - h)
     spread_flat(every, 0, 2)
-    climb_on(1)
-    step_right(1)
-    step_left(1)
-    climbed(0)
 
     mixed[0:5] = nn(w_zero[...].reshape(5 * local, 5 * C), flat_zero[:, 0:edges]).reshape(
         5, local, edges
@@ -508,7 +504,11 @@
     tally[...] = jnp.broadcast_to(total, tally.shape)
     counted = [net.copy(tally, tallies.at[i], d) for i, d in enumerate(chan_peers)]
 
+    climb_on(1)
     climb(2)
+    climbed(0)
+    step_right(1)
+    step_left(1)
 
     scale = weight[...] * inverse
     for j in range(19):

time: 74.2 us -> 74 us (level)
  no operation moved by 1% of the time
where the time goes in v6:
time: 74 us; the launch traced here: 73.9 us
  Pallas kernels  73.3 us (99%)
    pallas_call x1, Pallas kernels, shards(): pl.pallas_call(layer_kernel, name='layer', out_shape=[jax.ShapeDtypeStruc...  72 us

profile of v6, /device:TPU:1, one launch (start us, length us, event | category | flops | bytes accessed | tf_op | source)
XLA Modules:
  0.0 73.9 jit_solution(7785968009942549381)
XLA Ops:
  0.6 72.0 %layer.1 = (bf16[25,64,128]{2,1,0:T(8,128)(2,1)S(1)}, bf16[25,64,128]{2,1,0:T(8,128)(2,1)S(1)}, f32[80,384]{1,0:T(8,128)S(1)}, f32[64,512]{1,0:T(8,128)S(1)}, f32[48,384]{1,0:T(8,128)S(1)}) custom-call(bf16[25,64,128]{2,1,0:T(8,128)(2,1)} %embed_hbm.1, bf16[25,64,128]{2,1,0:T(8,128)(2,1)} %cotangent_hbm.1, f32[5,64]{1,0:T(8,128)} %gain_hbm.1, ...), custom_call_target="tpu_custom_call" | custom-call | tf_op jit(solution)/shard_map/layer/pallas_call | solution.py:683
  72.7 1.2 %finish.1 = (bf16[25,64,128]{2,1,0:T(8,128)(2,1)}, bf16[25,64,128]{2,1,0:T(8,128)(2,1)}, f32[5,64,80]{2,1,0:T(8,128)}, f32[2,4,64,64]{3,2,1,0:T(8,128)}, f32[2,3,48,64]{3,2,1,0:T(8,128)}) custom-call(bf16[25,64,128]{2,1,0:T(8,128)(2,1)S(1)} %get-tuple-element.15.update_in, bf16[25,64,128]{2,1,0:T(8,128)(2,1)S(1)} %get-tuple-element.16.grad_in, ...), custom_call_target="tpu_custom_call" | custom-call | tf_op jit(solution)/shard_map/finish/pallas_call | solution.py:705

commit v7 on v6

--- a/solution.py
+++ b/solution.py
@@ -479,6 +479,7 @@
     near_r[2].wait_recv()
     over_own[2].wait_recv()
     to_twin_core(2, h)
+    climbed(0)
     cross_l[2].wait_recv()
     over_cross[2].wait_recv()
     to_twin_core(2, 1 - h)
@@ -506,7 +507,6 @@
 
     climb_on(1)
     climb(2)
-    climbed(0)
     step_right(1)
     step_left(1)
 
@@ -573,9 +573,9 @@
             grad_embed[k] = (
                 (own[k] + settled[k]) * gain_l - embed[k].astype(F32) * factor
             ).astype(BF16)
-    for one in lines:
-        one.wait_recv()
     for p, out, width in ((0, sum_one, 512), (1, sum_zero, 384), (2, sum_two, 384)):
+        for one in lines[3 * p : 3 * p + 3]:
+            one.wait_recv()
         total = kept[p][...]
         for i in range(3):
             total = total + line[p][i].astype(F32)

time: 74 us -> 71.7 us (0.969)
  Pallas kernels: 73.3 us -> 71 us
    pallas_call x1, Pallas kernels: 72 us -> 69.8 us  [shards(): pl.pallas_call(layer_kernel, name='layer', out_shape=[jax.ShapeDtypeStruc...]
where the time goes in v7:
time: 71.7 us
  Pallas kernels  71 us (99%)
    pallas_call x1, Pallas kernels, shards(): pl.pallas_call(layer_kernel, name='layer', out_shape=[jax.ShapeDtypeStruc...  69.8 us

profile of v7, /device:TPU:1, one launch (start us, length us, event | category | flops | bytes accessed | tf_op | source)
XLA Modules:
  0.0 71.7 jit_solution(10742434016545320451)
XLA Ops:
  0.6 69.8 %layer.1 = (bf16[25,64,128]{2,1,0:T(8,128)(2,1)S(1)}, bf16[25,64,128]{2,1,0:T(8,128)(2,1)S(1)}, f32[80,384]{1,0:T(8,128)S(1)}, f32[64,512]{1,0:T(8,128)S(1)}, f32[48,384]{1,0:T(8,128)S(1)}) custom-call(bf16[25,64,128]{2,1,0:T(8,128)(2,1)} %embed_hbm.1, bf16[25,64,128]{2,1,0:T(8,128)(2,1)} %cotangent_hbm.1, f32[5,64]{1,0:T(8,128)} %gain_hbm.1, ...), custom_call_target="tpu_custom_call" | custom-call | tf_op jit(solution)/shard_map/layer/pallas_call | solution.py:683
  70.4 1.2 %finish.1 = (bf16[25,64,128]{2,1,0:T(8,128)(2,1)}, bf16[25,64,128]{2,1,0:T(8,128)(2,1)}, f32[5,64,80]{2,1,0:T(8,128)}, f32[2,4,64,64]{3,2,1,0:T(8,128)}, f32[2,3,48,64]{3,2,1,0:T(8,128)}) custom-call(bf16[25,64,128]{2,1,0:T(8,128)(2,1)S(1)} %get-tuple-element.15.update_in, bf16[25,64,128]{2,1,0:T(8,128)(2,1)S(1)} %get-tuple-element.16.grad_in, ...), custom_call_target="tpu_custom_call" | custom-call | tf_op jit(solution)/shard_map/finish/pallas_call | solution.py:705
